TPU v7x, 32 devices: a whole 2x2x4 slice. The times are simulated.
32 devices in a mesh: pole: 4 (over y, core), dom: 8 (over z, x).
Axes of the slice: x: 2, y: 2, z: 4, core: 2. Of those that a mesh axis runs over, the one named last changes fastest.
Arguments:
- initial_block: bfloat16 [8, 8, 512, 256], P('dom'), may hold values from -24 to 24
- coupling: bfloat16 [8, 8, 512, 512], P('dom'), may hold values from -0.125 to 0.125
- pivots: bfloat16 [4, 8, 8, 2, 512, 512], P('pole', 'dom'), may hold values from -0.125 to 0.125
- interface: bfloat16 [4, 8, 3, 2, 512, 512], P('pole', 'dom'), may hold values from -0.1875 to 0.1875
- pole_values: float32 [4, 4], P('pole'), may hold values from 0.5 to 1.5
Outputs:
- filtered_basis: float32 [8, 8, 512, 256], P('dom', 'pole')
- rayleigh: float32 [256, 256], replicated
All inputs are finite; a program needn't handle non-finite values.
Results may differ from a plain program's by a relative error of at most 0.008.
Values sent between devices are 32-bit elements; how exact they have to be, the bound alone decides.
No kernel may reach another device: no remote copies, remote signals or barrier semaphores. Data moves between devices by JAX's collectives and lax.ppermute only.
A program may use at most 192 MiB of HBM per device.

v0:
```python
import jax
import jax.numpy as jnp
from jax import lax
from jax.sharding import PartitionSpec as P

B = 512
M = 256


def shifted(x, axis, by):
    length = lax.axis_size(axis)
    pairs = [(i, i + by) for i in range(length) if 0 <= i + by < length]
    return lax.ppermute(x, axis, pairs)


def lower_solve(factor, right_side):
    return lax.linalg.triangular_solve(factor, right_side, left_side=True, lower=True)


def complex_product(matrix, vectors):
    block_order = matrix.shape[1]
    half_width = vectors.shape[1] // 2
    stacked = matrix.reshape(2 * block_order, block_order)
    stacked_out = jnp.dot(stacked, vectors.astype(jnp.bfloat16), preferred_element_type=jnp.float32)
    real_part = stacked_out[:block_order, :half_width] - stacked_out[block_order:, half_width:]
    imag_part = stacked_out[:block_order, half_width:] + stacked_out[block_order:, :half_width]
    return jnp.concatenate([real_part, imag_part], axis=1)


def real_product(matrix, vectors):
    return jnp.dot(matrix, vectors.astype(jnp.bfloat16), preferred_element_type=jnp.float32)


def transposed_product(matrix, vectors):
    return lax.dot_general(
        matrix,
        vectors.astype(jnp.bfloat16),
        (((0,), (0,)), ((), ())),
        preferred_element_type=jnp.float32,
    )


def inner_products(left, right_side):
    return lax.dot_general(
        left,
        right_side,
        (((0,), (0,)), ((), ())),
        precision=lax.Precision.HIGHEST,
        preferred_element_type=jnp.float32,
    )


def partition_solve(inverse, coupled, source):
    previous = jnp.roll(coupled, 1, axis=0)
    initial = jnp.zeros(source.shape[1:], jnp.float32)

    def forward_step(carried, members):
        block_inverse, given, couple_prev = members
        result = complex_product(block_inverse, given + transposed_product(couple_prev, carried))
        return (result, result)

    unused, forward = lax.scan(forward_step, initial, (inverse, source, previous))

    def backward_step(carried, members):
        block_inverse, partial_value, couple_next = members
        result = partial_value + complex_product(block_inverse, real_product(couple_next, carried))
        return (result, result)

    unused, backward = lax.scan(backward_step, initial, (inverse, forward, coupled), reverse=True)
    return backward


def on_device(initial_block, coupling, pivots, interface, pole_values):
    blocks = coupling.shape[1]
    coupled = coupling[0]
    inverse = pivots[0, 0]
    factors = interface[0, 0]
    real_start = initial_block[0].astype(jnp.float32)
    source = jnp.concatenate([real_start, jnp.zeros_like(real_start)], axis=-1)
    first = partition_solve(inverse, coupled, source)
    bottom = first[blocks - 1]
    top = first[0]
    top_next = shifted(top, "dom", -1)
    below = complex_product(factors[0], bottom) - complex_product(factors[1], top_next)
    topmost = lax.axis_index("dom") == lax.axis_size("dom") - 1
    above = jnp.where(
        topmost, jnp.zeros_like(top_next), top_next - complex_product(factors[2], below)
    )
    link = coupled[blocks - 1]
    lifted = transposed_product(link, below)
    arriving = shifted(lifted, "dom", 1)
    update = source.at[0].add(arriving)
    update = update.at[blocks - 1].add(real_product(link, above))
    second = partition_solve(inverse, coupled, update)
    real_z = pole_values[0, 0]
    imag_z = pole_values[0, 1]
    real_w = pole_values[0, 2]
    imag_w = pole_values[0, 3]
    real_x = second[..., :M]
    imag_x = second[..., M:]
    filtered_term = real_w * real_x - imag_w * imag_x
    shifted_term = (
        (real_w * real_z - imag_w * imag_z) * real_x
        - (real_w * imag_z + imag_w * real_z) * imag_x
        - real_w * real_start
    )
    count = blocks // lax.axis_size("pole")
    summed = lax.psum(filtered_term, "pole")
    offset = lax.axis_index("pole") * count
    own_rows = lax.dynamic_slice_in_dim(summed, offset, count, 0).reshape(count * B, M)
    gram_part = inner_products(own_rows, own_rows)
    projected_part = inner_products(
        summed.reshape(blocks * B, M), shifted_term.reshape(blocks * B, M)
    )
    gram_total, projected_total = lax.psum((gram_part, projected_part), ("pole", "dom"))
    row_total = blocks * B * lax.axis_size("dom")
    gram = gram_total / row_total
    projected = projected_total / row_total
    factor = jnp.linalg.cholesky(gram)
    filtered_basis = lower_solve(factor, own_rows.T).T.reshape(1, count, B, M)
    middle = lower_solve(factor, projected)
    rayleigh = lower_solve(factor, middle.T).T
    return (filtered_basis, rayleigh)


def solution(mesh):
    in_specs = (
        P("dom", None, None, None),
        P("dom", None, None, None),
        P("pole", "dom", None, None, None, None),
        P("pole", "dom", None, None, None, None),
        P("pole", None),
    )
    out_specs = (P("dom", "pole", None, None), P())
    return jax.shard_map(
        on_device, mesh=mesh, in_specs=in_specs, out_specs=out_specs, check_vma=False
    )
```

profile of v0, /device:TPU:0, one launch (start us, length us, event | category | flops | bytes accessed | tf_op | source)
XLA Modules:
  0.0 687.4 jit_solution(11109018124211285651)
XLA Ops:
  7.2 4.2 slice_bitcast_fusion
  12.5 2.9 copy.17
  18.0 4.2 concatenate.76
  24.6 4.3 broadcast.158.clone.2
  29.7 65.2 %while.65 = (s32[]{:T(128)}, bf16[512,512]{0,1:T(8,128)(2,1)}, f32[8,512,512]{1,2,0:T(8,128)}, bf16[8,2,512,512]{3,2,1,0:T(8,128)(2,1)}, f32[8,512,512]{1,2,0:T(8,128)}, /*index=5*/bf16[8,512,512]{2,1,0:T(8,128)(2,1)}, s32[]{:T(128)}) while((s32[]{:T(128)}, bf16[512,512]{0,1:T(8,128)(2,1)}, f32[8,512,512]{1,2,0:T(8,128)}, ...), condition=%wide.region_1.2_spmd, body=%wide.region_0.1_spmd.sunk | while | flops 806617088 | bytes 17302612 | solution.py:62
  41.8 2.7 fusion.145
  49.9 2.7 fusion.145
  58.1 2.7 fusion.145
  66.3 2.7 fusion.145
  90.7 2.7 fusion.145
  95.0 4.3 broadcast.158.clone.1
  99.3 67.7 %while.68 = (s32[]{:T(128)}, bf16[512,512]{0,1:T(8,128)(2,1)}, f32[8,512,512]{1,2,0:T(8,128)}, f32[8,512,512]{1,2,0:T(8,128)}, bf16[8,2,512,512]{3,2,1,0:T(8,128...) while((s32[]{:T(128)}, bf16[512,512]{0,1:T(8,128)(2,1)}, ...), condition=%wide.region_3.4_spmd.clone, body=%wide.region_2.3_spmd.clone.sunk | while | flops 807403520 | bytes 15204483 | solution.py:69
  173.8 22.5 %collective-permute-done = f32[512,512]{0,1:T(8,128)S(1)} collective-permute-done((f32[512,512]{0,1:T(8,128)S(1)}, f32[512,512]{0,1:T(8,128)S(1)}, u32[]{:S(2)}, u32[]{:S(2)}) %collective-permute-start) | collective-permute-done | bytes 1048608 | tf_op jit(solution)/shard_map/ppermute | solution.py:13
  200.0 5.8 collective-permute-start.1
  207.5 19.0 %collective-permute-done.1 = f32[512,512]{0,1:T(8,128)} collective-permute-done((f32[512,512]{0,1:T(8,128)}, f32[512,512]{0,1:T(8,128)}, u32[]{:S(2)}, u32[]{:S(2)}) %collective-permute-start.1) | collective-permute-done | bytes 1048608 | tf_op jit(solution)/shard_map/ppermute | solution.py:13
  228.8 2.9 fusion.66
  231.7 4.3 broadcast.158.clone
  236.9 65.4 %while.66 = (s32[]{:T(128)}, bf16[512,512]{0,1:T(8,128)(2,1)}, f32[8,512,512]{1,2,0:T(8,128)}, bf16[8,2,512,512]{3,2,1,0:T(8,128)(2,1)}, f32[8,512,512]{1,2,0:T(8,128)}, /*index=5*/bf16[8,512,512]{2,1,0:T(8,128)(2,1)}, s32[]{:T(128)}) while((s32[]{:T(128)}, bf16[512,512]{0,1:T(8,128)(2,1)}, f32[8,512,512]{1,2,0:T(8,128)}, ...), condition=%wide.region_5.6_spmd, body=%wide.region_4.5_spmd.sunk | while | flops 806617088 | bytes 17302612 | solution.py:62
  257.0 2.7 fusion.149
  265.2 2.7 fusion.149
  289.9 2.7 fusion.149
  302.3 4.3 broadcast.158
  306.6 67.7 %while.69 = (s32[]{:T(128)}, bf16[512,512]{0,1:T(8,128)(2,1)}, f32[8,512,512]{1,2,0:T(8,128)}, f32[8,512,512]{1,2,0:T(8,128)}, bf16[8,2,512,512]{3,2,1,0:T(8,128...) while((s32[]{:T(128)}, bf16[512,512]{0,1:T(8,128)(2,1)}, ...), condition=%wide.region_7.8_spmd.clone, body=%wide.region_6.7_spmd.clone.sunk | while | flops 807403520 | bytes 15204483 | solution.py:69
  374.3 7.7 %multiply_subtract_fusion = f32[8,512,256]{1,2,0:T(8,128)} fusion(f32[8,512,512]{1,2,0:T(8,128)} %get-tuple-element.338, f32[]{:T(128)} %bitcast.27, f32[]{:T(128)} %bitcast.8), kind=kLoop, calls=%fused_computation.67 | loop fusion | flops 3145728 | bytes 12582920 | tf_op jit(solution)/shard_map/sub | solution.py:101
  387.2 81.8 %all-reduce.6.cloned.1.call-done = f32[8,512,256]{1,2,0:T(8,128)} async-done(((f32[8,512,256]{1,2,0:T(8,128)}), f32[8,512,256]{1,2,0:T(8,128)}) %all-reduce.6.cloned.1.call-update) | async-done | bytes 4194320 | tf_op jit(solution)/shard_map/psum | solution.py:108
  472.1 9.1 %fusion.61 = f32[256,256]{0,1:T(8,128)} fusion(f32[8,512,256]{1,2,0:T(8,128)S(1)} %copy-done.5, f32[8,512,512]{1,2,0:T(8,128)} %get-tuple-element.338, f32[]{:T(128)S(6)} %add.171, f32[]{:T(128)S(6)} %sub.71, f32[]{:T(128)} %bitcast.8, bf16[1,8,512,256]{2,3,1,0:T(8,128)(2,1)S(1)} %copy-done.3), kind=kOutput, calls=%fused_computation.82 | convolution fusion | flops 3227516928 | bytes 14942220 | tf_op jit(solution)/shard_map/dot_general | solution.py:44
  481.6 129.2 %all-reduce.8.cloned.1.call-done = (f32[256,256]{0,1:T(8,128)}, f32[256,256]{0,1:T(8,128)}) async-done(((f32[256,256]{0,1:T(8,128)}, f32[256,256]{0,1:T(8,128)}), (f32[256,256]{0,1:T(8,128)}, f32[256,256]{0,1:T(8,128)})) %all-reduce.8.cloned.1.call-update) | async-done | bytes 524304 | tf_op jit(solution)/shard_map/psum | solution.py:115
  613.1 11.7 %cholesky.50 = f32[128,128]{1,0:T(8,128)S(1)} custom-call(f32[128,128]{1,0:T(8,128)S(1)} %cholesky.118), custom_call_target="Cholesky" | custom-call | tf_op jit(solution)/shard_map/jit(cholesky)/cholesky | solution.py:119
  624.8 10.1 %custom-call.17 = f32[1,128,128]{1,2,0:T(8,128)S(1)} custom-call(f32[1,128,128]{2,1,0:T(8,128)S(1)} %get-tuple-element.517), custom_call_target="InvertDiagBlocksLowerTriangular" | custom-call | tf_op jit(solution)/shard_map/jit(cholesky)/cholesky | solution.py:119
  635.4 11.7 %cholesky.105 = f32[128,128]{1,0:T(8,128)S(1)} custom-call(f32[128,128]{1,0:T(8,128)S(1)} %convolution_subtract_fusion.3), custom_call_target="Cholesky" | custom-call | tf_op jit(solution)/shard_map/jit(cholesky)/cholesky | solution.py:119
  649.8 4.0 while.67
  653.8 19.7 %custom-call.18 = f32[2,128,128]{1,2,0:T(8,128)S(1)} custom-call(f32[2,128,128]{2,1,0:T(8,128)S(1)} %get-tuple-element.354), custom_call_target="InvertDiagBlocksLowerTriangular" | custom-call | tf_op jit(solution)/shard_map/triangular_solve | solution.py:17
  (244 shorter events, 284.7 us)
Async XLA Ops:
  7.2 461.8 %all-reduce.6.cloned.1.call-start = ((), (), s32[]{:S(2)}) async-start(), calls=%async_computation | async-start | bytes 8388608 | tf_op jit(solution)/shard_map/psum | solution.py:108
  15.4 6.9 %copy-start.2 = (bf16[1,8,512,256]{2,3,1,0:T(8,128)(2,1)}, bf16[1,8,512,256]{2,3,1,0:T(8,128)(2,1)S(1)}, u32[]{:S(2)}) copy-start(bf16[1,8,512,256]{2,3,1,0:T(8,128)(2,1)S(1)} %copy.17) | copy-start | bytes 6291460
  15.9 2.1 copy-start
  18.0 4.2 copy-start.4
  168.3 28.0 %collective-permute-start = (f32[512,512]{0,1:T(8,128)S(1)}, f32[512,512]{0,1:T(8,128)S(1)}, u32[]{:S(2)}, u32[]{:S(2)}) collective-permute-start(f32[512,512]{0,1:T(8,128)S(1)} %slice_bitcast_fusion.1), channel_id=1, source_target_pairs={{1,0},{2,1},{3,2},{4,3},{5,4},{6,5},{7,6},{9,8},{10,9},{11,10},{12... | collective-permute-start | bytes 3145736 | tf_op jit(solution)/shard_map/ppermute | solution.py:13
  197.1 8.8 %copy-start.6 = (f32[1,4]{1,0:T(1,128)S(1)}, f32[1,4]{1,0:T(1,128)}, u32[]{:S(2)}) copy-start(f32[1,4]{1,0:T(1,128)} %param.23) | copy-start | bytes 52
  200.0 26.4 %collective-permute-start.1 = (f32[512,512]{0,1:T(8,128)}, f32[512,512]{0,1:T(8,128)}, u32[]{:S(2)}, u32[]{:S(2)}) collective-permute-start(f32[512,512]{0,1:T(8,128)} %convolution_bitcast_fusion.4), channel_id=1, source_target_pairs={{0,1},{1,2},{2,3},{3,4},{4,5},{5,6},{6,7},{8,9},{9,10},{10,11},{11... | collective-permute-start | bytes 3145736 | tf_op jit(solution)/shard_map/ppermute | solution.py:13
  205.8 20.6 %copy-start.1 = (f32[8,512,256]{1,2,0:T(8,128)S(1)}, f32[8,512,256]{1,2,0:T(8,128)}, u32[]{:S(2)}) copy-start(f32[8,512,256]{1,2,0:T(8,128)} %copy-done) | copy-start | bytes 12582916
  382.0 90.2 %copy-start.3 = (bf16[1,8,512,256]{2,3,1,0:T(8,128)(2,1)S(1)}, bf16[1,8,512,256]{2,3,1,0:T(8,128)(2,1)}, u32[]{:S(2)}) copy-start(bf16[1,8,512,256]{2,3,1,0:T(8,128)(2,1)} %copy-done.2) | copy-start | bytes 6291460
  382.0 228.8 %all-reduce.8.cloned.1.call-start = ((), (), s32[]{:S(2)}) async-start(), calls=%async_computation.1 | async-start | bytes 1048576 | tf_op jit(solution)/shard_map/psum | solution.py:115
  469.0 3.2 copy-start.5
Sparse Core Ops, SparseCore 0:
  382.1 86.7 all-reduce.5
  481.4 129.4 all-reduce.7
where the time goes:
time: 699 us; the launch traced here: 687 us
  waiting for transfers between devices  253 us (36%)
  other arithmetic  173 us (25%)
  local copies, waits for them, and re-layouts  128 us (18%)
  matrix products  104 us (15%)
  between operations  21 us (3%)
  starting transfers between devices  7.34 us (1%)
    psum x1, waiting for transfers between devices, on_device(): lax.psum((gram_part, projected_part), ('pole', 'dom'))  129 us
    dot_general x35, matrix products, complex_product(): jnp.dot(stacked, vectors.astype(jnp.bfloat16), preferred_element_type=jnp...  83.1 us
    dynamic_slice x64, local copies, waits for them, and re-layouts, partition_solve(): lax.scan(forward_step, initial, (inverse, source, previous))  82.9 us
    psum x1, waiting for transfers between devices, on_device(): summed = lax.psum(filtered_term, 'pole')  81.8 us
    dynamic_update_slice x32, other arithmetic, partition_solve(): lax.scan(forward_step, initial, (inverse, source, previous))  60.9 us
    ppermute x2, waiting for transfers between devices, shifted(): return lax.ppermute(x, axis, pairs)  41.5 us
    add x16, other arithmetic, backward_step(): partial_value + complex_product(block_inverse, real_product(couple_next,...  35.2 us
    another operation x7, other arithmetic, on_device(): factor = jnp.linalg.cholesky(gram)  34.8 us
  transfers between devices with their start and end apart: 4, of which 4 were waited for; matrix products, arithmetic and copies ran while one was open for 1% of the time, Pallas kernels for 0%

commit v1 on v0

v1 whole, which is shorter than its diff:
```python
import functools
import jax
import jax.numpy as jnp
from jax import lax
from jax.experimental import pallas as pl
from jax.experimental.pallas import tpu as pltpu
from jax.sharding import PartitionSpec as P

F32 = jnp.float32
BF16 = jnp.bfloat16
LANES = 128


def shifted(x, axis, by):
    length = lax.axis_size(axis)
    pairs = [(i, i + by) for i in range(length) if 0 <= i + by < length]
    return lax.ppermute(x, axis, pairs)


def flipped(x, axis, mask):
    return lax.ppermute(x, axis, [(i, i ^ mask) for i in range(lax.axis_size(axis))])


def complex_apply(stacked, vectors):
    order = stacked.shape[0] // 2
    width = vectors.shape[1] // 2
    out = jnp.dot(stacked, vectors.astype(BF16), preferred_element_type=F32)
    real = out[:order, :width] - out[order:, width:]
    imag = out[:order, width:] + out[order:, :width]
    return jnp.concatenate([real, imag], axis=1)


def real_apply(matrix, vectors):
    return jnp.dot(matrix, vectors.astype(BF16), preferred_element_type=F32)


def transposed_apply(matrix, vectors):
    return lax.dot_general(
        matrix, vectors.astype(BF16), (((0,), (0,)), ((), ())), preferred_element_type=F32
    )


def block_copies(k, lane, f_hbm, g_hbm, u_hbm, fv, gv, uv, sem):
    width = fv.shape[2]
    return (
        pltpu.make_async_copy(f_hbm.at[k, :, pl.ds(lane, width)], fv.at[k], sem.at[0, k]),
        pltpu.make_async_copy(g_hbm.at[k], gv.at[k], sem.at[1, k]),
        pltpu.make_async_copy(u_hbm.at[k], uv.at[k], sem.at[2, k]),
    )


def first_kernel(lane, f_hbm, g_hbm, u_hbm, s_ref, top_ref, sb_ref, fv, gv, uv, ut, hold, sem):
    blocks = gv.shape[0]
    copies = functools.partial(
        block_copies, lane=lane, f_hbm=f_hbm, g_hbm=g_hbm, u_hbm=u_hbm, fv=fv, gv=gv, uv=uv, sem=sem
    )
    for k in range(blocks):
        for copy in copies(k):
            copy.start()
    order = uv.shape[1]
    for copy in copies(0):
        copy.wait()
    out = jnp.dot(gv[0], fv[0], preferred_element_type=F32)
    hold[0] = jnp.concatenate([out[:order], out[order:]], axis=1)
    ut[0] = uv[0].T

    def forward(k, carry):
        for copy in copies(k):
            copy.wait()
        coupled = real_apply(ut[(k + 1) % 2], hold[k - 1])
        given = fv[k].astype(F32)
        hold[k] = complex_apply(
            gv[k], coupled + jnp.concatenate([given, jnp.zeros_like(given)], axis=1)
        )
        ut[k % 2] = uv[k].T
        return carry

    lax.fori_loop(1, blocks, forward, 0)
    sb_ref[...] = complex_apply(s_ref[...], hold[blocks - 1])

    def backward(i, carry):
        k = blocks - 2 - i
        hold[k] = hold[k] + complex_apply(gv[k], real_apply(uv[k], hold[k + 1]))
        return carry

    lax.fori_loop(0, blocks - 1, backward, 0)
    top_ref[...] = hold[0]


def first_solve(chunk, width, source, inverse, coupled, s_factor):
    blocks, stacked, order = inverse.shape
    tip = jax.ShapeDtypeStruct((order, 2 * width), F32)
    hbm = pl.BlockSpec(memory_space=pl.ANY)
    vmem = pl.BlockSpec(memory_space=pltpu.VMEM)
    flops = 2 * order * order * 2 * width * (5 * blocks - 3)
    return pl.pallas_call(
        functools.partial(first_kernel, chunk * width),
        out_shape=(tip, tip),
        in_specs=[hbm, hbm, hbm, vmem],
        out_specs=(vmem, vmem),
        scratch_shapes=[
            pltpu.VMEM((blocks, order, width), BF16),
            pltpu.VMEM((blocks, stacked, order), BF16),
            pltpu.VMEM((blocks, order, order), BF16),
            pltpu.VMEM((2, order, order), BF16),
            pltpu.VMEM((blocks, order, 2 * width), F32),
            pltpu.SemaphoreType.DMA((3, blocks)),
        ],
        cost_estimate=pl.CostEstimate(flops=flops, transcendentals=0, bytes_accessed=12 * 2**20),
        name="first_solve",
    )(source, inverse, coupled, s_factor)


def interface_kernel(last_ref, sb_ref, next_ref, k_ref, w_ref, link_ref, lifted_ref, added_ref):
    top_next = next_ref[...]
    below = sb_ref[...] - complex_apply(k_ref[...], top_next)
    lifted_ref[...] = transposed_apply(link_ref[...], below)
    above = top_next - complex_apply(w_ref[...], below)
    above = jnp.where(last_ref[0] == 1, jnp.zeros_like(above), above)
    added_ref[...] = real_apply(link_ref[...], above)


def interface_step(topmost, s_times, top_next, k_factor, w_factor, link):
    shape = jax.ShapeDtypeStruct(top_next.shape, F32)
    order, width = top_next.shape
    vmem = pl.BlockSpec(memory_space=pltpu.VMEM)
    return pl.pallas_call(
        interface_kernel,
        out_shape=(shape, shape),
        in_specs=[pl.BlockSpec(memory_space=pltpu.SMEM)] + [vmem] * 5,
        out_specs=(vmem, vmem),
        cost_estimate=pl.CostEstimate(
            flops=12 * order * order * width, transcendentals=0, bytes_accessed=4 * 2**20
        ),
        name="interface_step",
    )(topmost, s_times, top_next, k_factor, w_factor, link)


def second_kernel(
    lane, owners, place_ref, scale_ref, f_hbm, g_hbm, u_hbm, arrive_ref, added_ref,
    keep_y, keep_z, send_y, send_z, fv, gv, uv, ut, hold, sem,
):
    blocks = gv.shape[0]
    count = blocks // owners
    copies = functools.partial(
        block_copies, lane=lane, f_hbm=f_hbm, g_hbm=g_hbm, u_hbm=u_hbm, fv=fv, gv=gv, uv=uv, sem=sem
    )
    for k in range(blocks):
        for copy in copies(k):
            copy.start()
    width = fv.shape[2]

    def given(k):
        real = fv[k].astype(F32)
        return jnp.concatenate([real, jnp.zeros_like(real)], axis=1)

    for copy in copies(0):
        copy.wait()
    hold[0] = complex_apply(gv[0], given(0) + arrive_ref[...])
    ut[0] = uv[0].T

    def forward(k, carry):
        for copy in copies(k):
            copy.wait()
        coupled = real_apply(ut[(k + 1) % 2], hold[k - 1])
        hold[k] = complex_apply(gv[k], given(k) + coupled)
        ut[k % 2] = uv[k].T
        return carry

    lax.fori_loop(1, blocks - 1, forward, 0)
    last = blocks - 1
    for copy in copies(last):
        copy.wait()
    coupled = real_apply(ut[(last + 1) % 2], hold[last - 1])
    hold[last] = complex_apply(gv[last], (given(last) + added_ref[...]) + coupled)

    wr, wi, zwr, zwi = scale_ref[0], scale_ref[1], scale_ref[2], scale_ref[3]
    low = place_ref[0]
    high = place_ref[1]

    def emit(k, x):
        real, imag = x[:, :width], x[:, width:]
        y = wr * real - wi * imag
        z = zwr * real - zwi * imag - wr * fv[k].astype(F32)
        owner = k // count
        slot = ((owner // 2) ^ high) * count + k % count

        @pl.when(owner % 2 == low)
        def _():
            keep_y[slot] = y
            keep_z[slot] = z

        @pl.when(owner % 2 != low)
        def _():
            send_y[slot] = y
            send_z[slot] = z

    emit(last, hold[last])

    def backward(i, carry):
        k = blocks - 2 - i
        x = hold[k] + complex_apply(gv[k], real_apply(uv[k], hold[k + 1]))
        hold[k] = x
        emit(k, x)
        return carry

    lax.fori_loop(0, blocks - 1, backward, 0)


def second_solve(chunk, width, owners, place, scales, source, inverse, coupled, arriving, added):
    blocks, stacked, order = inverse.shape
    part = jax.ShapeDtypeStruct((blocks // 2, order, width), F32)
    hbm = pl.BlockSpec(memory_space=pl.ANY)
    vmem = pl.BlockSpec(memory_space=pltpu.VMEM)
    smem = pl.BlockSpec(memory_space=pltpu.SMEM)
    flops = 2 * order * order * 2 * width * (5 * blocks - 3)
    return pl.pallas_call(
        functools.partial(second_kernel, chunk * width, owners),
        out_shape=(part,) * 4,
        in_specs=[smem, smem, hbm, hbm, hbm, vmem, vmem],
        out_specs=(vmem,) * 4,
        scratch_shapes=[
            pltpu.VMEM((blocks, order, width), BF16),
            pltpu.VMEM((blocks, stacked, order), BF16),
            pltpu.VMEM((blocks, order, order), BF16),
            pltpu.VMEM((2, order, order), BF16),
            pltpu.VMEM((blocks, order, 2 * width), F32),
            pltpu.SemaphoreType.DMA((3, blocks)),
        ],
        cost_estimate=pl.CostEstimate(flops=flops, transcendentals=0, bytes_accessed=16 * 2**20),
        name="second_solve",
    )(place, scales, source, inverse, coupled, arriving, added)


def lower_solve(factor, right_side):
    return lax.linalg.triangular_solve(factor, right_side, left_side=True, lower=True)


def inner_products(left, right_side):
    return lax.dot_general(
        left,
        right_side,
        (((0,), (0,)), ((), ())),
        precision=lax.Precision.HIGHEST,
        preferred_element_type=F32,
    )


def summed_everywhere(x, steps, far):
    kept = []
    for axis, mask in steps:
        half = x.shape[0] // 2
        bit = (lax.axis_index(axis) // mask) % 2
        mine = lax.dynamic_slice_in_dim(x, bit * half, half, 0)
        other = lax.dynamic_slice_in_dim(x, (1 - bit) * half, half, 0)
        x = mine + flipped(other, axis, mask)
        kept.append(bit)
    axis, masks = far
    x = x + sum(flipped(x, axis, mask) for mask in masks)
    for (axis, mask), bit in zip(reversed(steps), reversed(kept)):
        other = flipped(x, axis, mask)
        x = jnp.where(bit == 0, jnp.concatenate([x, other]), jnp.concatenate([other, x]))
    return x


def on_device(initial_block, coupling, pivots, interface, pole_values):
    blocks = coupling.shape[1]
    order = coupling.shape[2]
    vectors = initial_block.shape[3]
    width = min(LANES, vectors)
    owners = lax.axis_size("pole")
    parts = lax.axis_size("dom")
    count = blocks // owners
    source = initial_block[0]
    coupled = coupling[0]
    inverse = pivots[0, 0].reshape(blocks, 2 * order, order)
    factors = interface[0, 0].reshape(3, 2 * order, order)
    link = coupled[blocks - 1]
    pole = lax.axis_index("pole")
    dom = lax.axis_index("dom")
    topmost = (dom == parts - 1).astype(jnp.int32).reshape(1)
    place = jnp.stack([pole % 2, pole // 2]).astype(jnp.int32)
    real_z, imag_z, real_w, imag_w = (pole_values[0, i] for i in range(4))
    scales = jnp.stack(
        [real_w, imag_w, real_w * real_z - imag_w * imag_z, real_w * imag_z + imag_w * real_z]
    )
    chunks = vectors // width
    firsts = [first_solve(c, width, source, inverse, coupled, factors[0]) for c in range(chunks)]
    tops = [shifted(top, "dom", -1) for top, _ in firsts]
    middles = [
        interface_step(topmost, firsts[c][1], tops[c], factors[1], factors[2], link)
        for c in range(chunks)
    ]
    arrivals = [shifted(lifted, "dom", 1) for lifted, _ in middles]
    seconds = [
        second_solve(c, width, owners, place, scales, source, inverse, coupled, arrivals[c], middles[c][1])
        for c in range(chunks)
    ]

    def gathered(keep, send):
        part = keep + flipped(send, "pole", 1)
        mask = 2
        while mask < owners:
            half = part.shape[0] // 2
            part = part[:half] + flipped(part[half:], "pole", mask)
            mask *= 2
        return part.reshape(count * order, width)

    own_y = jnp.concatenate([gathered(s[0], s[2]) for s in seconds], axis=1)
    own_z = jnp.concatenate([gathered(s[1], s[3]) for s in seconds], axis=1)
    gram_part = inner_products(own_y, own_y)
    projected_part = inner_products(own_y, own_z)
    both = jnp.concatenate([gram_part, projected_part], axis=1)
    near = [("pole", 1 << i) for i in range(owners.bit_length() - 1)] + [("dom", 1)]
    both = summed_everywhere(both, near, ("dom", tuple(range(2, parts, 2))))
    row_total = blocks * order * parts
    gram = both[:, :vectors] / row_total
    projected = both[:, vectors:] / row_total
    factor = jnp.linalg.cholesky(gram)
    filtered_basis = lower_solve(factor, own_y.T).T.reshape(1, count, order, vectors)
    middle = lower_solve(factor, projected)
    rayleigh = lower_solve(factor, middle.T).T
    return (filtered_basis, rayleigh)


def solution(mesh):
    in_specs = (
        P("dom", None, None, None),
        P("dom", None, None, None),
        P("pole", "dom", None, None, None, None),
        P("pole", "dom", None, None, None, None),
        P("pole", None),
    )
    out_specs = (P("dom", "pole", None, None), P())
    return jax.shard_map(
        on_device, mesh=mesh, in_specs=in_specs, out_specs=out_specs, check_vma=False
    )
```

time: 699 us -> 308 us (0.44)
  waiting for transfers between devices: 253 us -> 83 us
  local copies, waits for them, and re-layouts: 128 us -> 17.8 us
  other arithmetic: 173 us -> 63.3 us
  matrix products: 104 us -> 8.38 us
  Pallas kernels: 0 us -> 84.9 us
  starting transfers between devices: 7.34 us -> 37.4 us
  between operations: 21 us -> 7.77 us
    psum x2 -> x0, waiting for transfers between devices: 211 us -> none  [the longest x1 129 us: on_device(): lax.psum((gram_part, projected_part), ('pole', 'dom'))]
    dot_general x37 -> x0, matrix products: 88.4 us -> none  [the longest x35 83.1 us: complex_product(): jnp.dot(stacked, vectors.astype(jnp.bfloat16), preferred_element_type=jnp...]
    pallas_call x0 -> x6, Pallas kernels: none -> 84.9 us  [the longest x2 44 us: second_solve(): pl.pallas_call(functools.partial(second_kernel, chunk * width, owners), o...]
    dynamic_slice x66 -> x2, local copies, waits for them, and re-layouts: 84.7 us -> 0.26 us  [summed_everywhere(): other = lax.dynamic_slice_in_dim(x, (1 - bit) * half, half, 0)]
    ppermute x0 -> x17, waiting for transfers between devices: none -> 83 us  [flipped(): lax.ppermute(x, axis, [(i, i ^ mask) for i in range(lax.axis_size(axis))])]
    dynamic_update_slice x32 -> x0, other arithmetic: 60.9 us -> none  [partition_solve(): lax.scan(forward_step, initial, (inverse, source, previous))]
    ppermute x2 -> x4, waiting for transfers between devices: 41.5 us -> 0.01 us  [shifted(): return lax.ppermute(x, axis, pairs)]
    add x16 -> x12, other arithmetic: 35.2 us -> 6.33 us  [the longest x4 4.73 us: gathered(): part = keep + flipped(send, 'pole', 1)]
  transfers between devices with their start and end apart: 4 -> 21, of which waited for: 4 -> 12; matrix products, arithmetic and copies ran while one was open for 1% -> 5% of each run, Pallas kernels for 0% -> 23%
where the time goes in v1:
time: 308 us; the launch traced here: 303 us
  Pallas kernels  84.9 us (28%)
  waiting for transfers between devices  83 us (27%)
  other arithmetic  63.3 us (21%)
  starting transfers between devices  37.4 us (12%)
  local copies, waits for them, and re-layouts  17.8 us (6%)
  matrix products  8.38 us (3%)
  between operations  7.77 us (3%)
    ppermute x17, waiting for transfers between devices, flipped(): lax.ppermute(x, axis, [(i, i ^ mask) for i in range(lax.axis_size(axis))])  83 us
    pallas_call x2, Pallas kernels, second_solve(): pl.pallas_call(functools.partial(second_kernel, chunk * width, owners), o...  44 us
    another operation x6, other arithmetic, on_device(): factor = jnp.linalg.cholesky(gram)  34.1 us
    pallas_call x2, Pallas kernels, first_solve(): pl.pallas_call(functools.partial(first_kernel, chunk * width), out_shape=...  31.5 us
    ppermute x17, starting transfers between devices, flipped(): lax.ppermute(x, axis, [(i, i ^ mask) for i in range(lax.axis_size(axis))])  23.8 us
    another operation x3, other arithmetic, lower_solve(): lax.linalg.triangular_solve(factor, right_side, left_side=True, lower=True)  19.7 us
    ppermute x4, starting transfers between devices, shifted(): return lax.ppermute(x, axis, pairs)  13.5 us
    pallas_call x2, Pallas kernels, interface_step(): pl.pallas_call(interface_kernel, out_shape=(shape, shape), in_specs=[pl.B...  9.37 us
  transfers between devices with their start and end apart: 21, of which 12 were waited for; matrix products, arithmetic and copies ran while one was open for 5% of the time, Pallas kernels for 23%

profile of v1, /device:TPU:0, one launch (start us, length us, event | category | flops | bytes accessed | tf_op | source)
XLA Modules:
  0.0 302.6 jit_solution(4680463296639403774)
XLA Ops:
  0.6 3.6 %fusion.28 = (bf16[1,1,1,2,512,512]{5,4,3,2,1,0:T(8,128)(2,1)}, bf16[1,1,1,2,512,512]{5,4,3,2,1,0:T(8,128)(2,1)}, bf16[1,1,1,2,512,512]{5,4,3,2,1,0:T(8,128)(2,1)}) fusion(bf16[1,1,3,2,512,512]{5,4,3,2,1,0:T(8,128)(2,1)} %param.10), kind=kLoop, calls=%fused_computation.74 | loop fusion | bytes 6291456 | tf_op jit(solution)/shard_map/slice | solution.py:291
  4.2 15.8 %first_solve.3 = (f32[512,256]{1,0:T(8,128)}, f32[512,256]{1,0:T(8,128)}) custom-call(bf16[8,512,256]{2,1,0:T(8,128)(2,1)} %bitcast.100, bf16[8,1024,512]{2,1,0:T(8,128)(2,1)} %bitcast.96, bf16[8,512,512]{2,1,0:T(8,128)(2,1)} %bitcast.92, bf16[1024,512]{1,0:T(8,128)(2,1)} %bitcast.90), custom_call_target="tpu_custom_call" | custom-call | flops 4966055936 | bytes 12582912 | tf_op jit(solution)/shard_map/first_solve/pallas_call | solution.py:96
  21.3 15.7 %first_solve.2 = (f32[512,256]{1,0:T(8,128)}, f32[512,256]{1,0:T(8,128)}) custom-call(bf16[8,512,256]{2,1,0:T(8,128)(2,1)} %bitcast.101, bf16[8,1024,512]{2,1,0:T(8,128)(2,1)} %bitcast.97, bf16[8,512,512]{2,1,0:T(8,128)(2,1)} %bitcast.93, bf16[1024,512]{1,0:T(8,128)(2,1)} %bitcast.91), custom_call_target="tpu_custom_call" | custom-call | flops 4966055936 | bytes 12582912 | tf_op jit(solution)/shard_map/first_solve/pallas_call | solution.py:96
  38.4 1.9 slice_bitcast_fusion.link_ref
  41.1 4.7 %interface_step.3 = (f32[512,256]{1,0:T(8,128)}, f32[512,256]{1,0:T(8,128)}) custom-call(s32[1]{0:T(128)} %bitcast.9.last_ref, f32[512,256]{1,0:T(8,128)} %get-tuple-element.25.sb_ref, f32[512,256]{1,0:T(8,128)} %copy-done.4, bf16[1024,512]{1,0:T(8,128)(2,1)} %bitcast.79, bf16[1024,512]{1,0:T(8,128)(2,1)} %bitcast.77, ...), custom_call_target="tpu_custom_call" | custom-call | flops 805306368 | bytes 4194304 | tf_op jit(solution)/shard_map/interface_step/pallas_call | solution.py:127
  45.7 6.1 %collective-permute-start.5 = (f32[512,256]{1,0:T(8,128)}, f32[512,256]{1,0:T(8,128)S(1)}, u32[]{:S(2)}, u32[]{:S(2)}) collective-permute-start(f32[512,256]{1,0:T(8,128)} %get-tuple-element.27), channel_id=1, source_target_pairs={{0,1},{1,2},{2,3},{3,4},{4,5},{5,6},{6,7},{8,9},{9,10},{10,11},{11... | collective-permute-start | bytes 1572872 | tf_op jit(solution)/shard_map/ppermute | solution.py:17
  59.0 4.7 %interface_step.2 = (f32[512,256]{1,0:T(8,128)}, f32[512,256]{1,0:T(8,128)}) custom-call(s32[1]{0:T(128)} %bitcast.9.last_ref, f32[512,256]{1,0:T(8,128)} %get-tuple-element.19.sb_ref, f32[512,256]{1,0:T(8,128)} %copy-done.3, bf16[1024,512]{1,0:T(8,128)(2,1)} %bitcast.80, bf16[1024,512]{1,0:T(8,128)(2,1)} %bitcast.78, ...), custom_call_target="tpu_custom_call" | custom-call | flops 805306368 | bytes 4194304 | tf_op jit(solution)/shard_map/interface_step/pallas_call | solution.py:127
  63.7 4.8 %collective-permute-start.1 = (f32[512,256]{1,0:T(8,128)}, f32[512,256]{1,0:T(8,128)S(1)}, u32[]{:S(2)}, u32[]{:S(2)}) collective-permute-start(f32[512,256]{1,0:T(8,128)} %get-tuple-element.21), channel_id=1, source_target_pairs={{0,1},{1,2},{2,3},{3,4},{4,5},{5,6},{6,7},{8,9},{9,10},{10,11},{11... | collective-permute-start | bytes 1572872 | tf_op jit(solution)/shard_map/ppermute | solution.py:17
  71.1 18.1 %second_solve.3 = (f32[4,512,128]{2,1,0:T(8,128)}, f32[4,512,128]{2,1,0:T(8,128)}, f32[4,512,128]{2,1,0:T(8,128)}, f32[4,512,128]{2,1,0:T(8,128)}) custom-call(s32[2]{0:T(128)} %pad_add_fusion.place_ref, f32[4]{0:T(128)} %pad_maximum_fusion.3.scale_ref, bf16[8,512,256]{2,1,0:T(8,128)(2,1)} %bitcast.102, bf16[8,1024,512]{2,1,0:T(8,128)(2,1)} %bitcast.98, ...), custom_call_target="tpu_custom_call" | custom-call | flops 4966055936 | bytes 16777216 | tf_op jit(solution)/shard_map/second_solve/pallas_call | solution.py:217
  90.2 25.9 %second_solve.2 = (f32[4,512,128]{2,1,0:T(8,128)}, f32[4,512,128]{2,1,0:T(8,128)}, f32[4,512,128]{2,1,0:T(8,128)}, f32[4,512,128]{2,1,0:T(8,128)}) custom-call(s32[2]{0:T(128)} %pad_add_fusion.place_ref, f32[4]{0:T(128)} %pad_maximum_fusion.3.scale_ref, bf16[8,512,256]{2,1,0:T(8,128)(2,1)} %bitcast.103, bf16[8,1024,512]{2,1,0:T(8,128)(2,1)} %bitcast.99, ...), custom_call_target="tpu_custom_call" | custom-call | flops 4966055936 | bytes 16777216 | tf_op jit(solution)/shard_map/second_solve/pallas_call | solution.py:217
  119.5 2.1 collective-permute-start.7
  124.3 2.1 collective-permute-start.11
  128.2 6.2 %collective-permute-done.7 = f32[2,512,128]{2,1,0:T(8,128)S(1)} collective-permute-done((f32[2,512,128]{2,1,0:T(8,128)S(1)}, f32[2,512,128]{2,1,0:T(8,128)S(1)}, u32[]{:S(2)}, u32[]{:S(2)}) %collective-permute-start.7) | collective-permute-done | bytes 524320 | tf_op jit(solution)/shard_map/ppermute | solution.py:21
  134.5 11.3 %collective-permute-done.3 = f32[2,512,128]{2,1,0:T(8,128)} collective-permute-done((f32[2,512,128]{2,1,0:T(8,128)}, f32[2,512,128]{2,1,0:T(8,128)}, u32[]{:S(2)}, u32[]{:S(2)}) %collective-permute-start.3) | collective-permute-done | bytes 524320 | tf_op jit(solution)/shard_map/ppermute | solution.py:21
  146.9 1.8 fusion.5
  148.7 8.2 %collective-permute-done.11 = f32[2,512,128]{2,1,0:T(8,128)S(1)} collective-permute-done((f32[2,512,128]{2,1,0:T(8,128)S(1)}, f32[2,512,128]{2,1,0:T(8,128)S(1)}, u32[]{:S(2)}, u32[]{:S(2)}) %collective-permute-start.11) | collective-permute-done | bytes 524320 | tf_op jit(solution)/shard_map/ppermute | solution.py:21
  156.9 10.6 %collective-permute-done.9 = f32[2,512,128]{2,1,0:T(8,128)S(1)} collective-permute-done((f32[2,512,128]{2,1,0:T(8,128)S(1)}, f32[2,512,128]{2,1,0:T(8,128)S(1)}, u32[]{:S(2)}, u32[]{:S(2)}) %collective-permute-start.9) | collective-permute-done | bytes 524320 | tf_op jit(solution)/shard_map/ppermute | solution.py:21
  167.6 1.8 fusion
  171.2 1.8 collective-permute-start.13
  173.0 6.6 %collective-permute-done.13 = f32[64,512]{0,1:T(8,128)S(1)} collective-permute-done((f32[64,512]{0,1:T(8,128)S(1)}, f32[64,512]{0,1:T(8,128)S(1)}, u32[]{:S(2)}, u32[]{:S(2)}) %collective-permute-start.13) | collective-permute-done | bytes 131104 | tf_op jit(solution)/shard_map/ppermute | solution.py:21
  179.9 8.9 %collective-permute-start.14 = (f32[32,512]{0,1:T(8,128)S(1)}, f32[32,512]{0,1:T(8,128)S(1)}, u32[]{:S(2)}, u32[]{:S(2)}) collective-permute-start(f32[32,512]{0,1:T(8,128)S(1)} %constant_dynamic-slice_fusion.1), channel_id=1, source_target_pairs={{0,1},{1,0},{2,3},{3,2},{4,5},{5,4},{6,7},{7,6},{8,9},{9,8},{10,11... | collective-permute-start | bytes 196616 | tf_op jit(solution)/shard_map/ppermute | solution.py:21
  188.8 5.8 %collective-permute-done.14 = f32[32,512]{0,1:T(8,128)S(1)} collective-permute-done((f32[32,512]{0,1:T(8,128)S(1)}, f32[32,512]{0,1:T(8,128)S(1)}, u32[]{:S(2)}, u32[]{:S(2)}) %collective-permute-start.14) | collective-permute-done | bytes 65568 | tf_op jit(solution)/shard_map/ppermute | solution.py:21
  194.7 2.4 collective-permute-start.17
  199.2 6.7 %collective-permute-done.17 = f32[32,512]{0,1:T(8,128)S(1)} collective-permute-done((f32[32,512]{0,1:T(8,128)S(1)}, f32[32,512]{0,1:T(8,128)S(1)}, u32[]{:S(2)}, u32[]{:S(2)}) %collective-permute-start.17) | collective-permute-done | bytes 65568 | tf_op jit(solution)/shard_map/ppermute | solution.py:21
  205.8 13.7 %collective-permute-done.16 = f32[32,512]{0,1:T(8,128)S(1)} collective-permute-done((f32[32,512]{0,1:T(8,128)S(1)}, f32[32,512]{0,1:T(8,128)S(1)}, u32[]{:S(2)}, u32[]{:S(2)}) %collective-permute-start.16) | collective-permute-done | bytes 65568 | tf_op jit(solution)/shard_map/ppermute | solution.py:21
  221.1 6.0 %collective-permute-done.18 = f32[32,512]{0,1:T(8,128)S(1)} collective-permute-done((f32[32,512]{0,1:T(8,128)S(1)}, f32[32,512]{0,1:T(8,128)S(1)}, u32[]{:S(2)}, u32[]{:S(2)}) %collective-permute-start.18) | collective-permute-done | bytes 65568 | tf_op jit(solution)/shard_map/ppermute | solution.py:21
  228.9 5.1 %collective-permute-done.19 = f32[64,512]{0,1:T(8,128)S(1)} collective-permute-done((f32[64,512]{0,1:T(8,128)S(1)}, f32[64,512]{0,1:T(8,128)S(1)}, u32[]{:S(2)}, u32[]{:S(2)}) %collective-permute-start.19) | collective-permute-done | bytes 131104 | tf_op jit(solution)/shard_map/ppermute | solution.py:21
  236.1 11.7 %cholesky.50 = f32[128,128]{1,0:T(8,128)S(1)} custom-call(f32[128,128]{1,0:T(8,128)S(1)} %cholesky.118), custom_call_target="Cholesky" | custom-call | tf_op jit(solution)/shard_map/jit(cholesky)/cholesky | solution.py:319
  247.8 10.0 %custom-call.17 = f32[1,128,128]{1,2,0:T(8,128)S(1)} custom-call(f32[1,128,128]{2,1,0:T(8,128)S(1)} %get-tuple-element.79), custom_call_target="InvertDiagBlocksLowerTriangular" | custom-call | tf_op jit(solution)/shard_map/jit(cholesky)/cholesky | solution.py:319
  258.3 11.7 %cholesky.105 = f32[128,128]{1,0:T(8,128)S(1)} custom-call(f32[128,128]{1,0:T(8,128)S(1)} %convolution_subtract_fusion.3), custom_call_target="Cholesky" | custom-call | tf_op jit(solution)/shard_map/jit(cholesky)/cholesky | solution.py:319
  272.0 3.8 %while.5 = (s32[]{:T(128)}, f32[256,256]{1,0:T(8,128)S(1)}, s32[2,2]{1,0:T(2,128)S(1)}, f32[2,128,128]{2,1,0:T(8,128)S(1)}, s32[]{:T(128)}) while((s32[]{:T(128)}, f32[256,256]{1,0:T(8,128)S(1)}, s32[2,2]{1,0:T(2,128)S(1)}, f32[2,128,128]{2,1,0:T(8,128)S(1)}, s32[]{:T(128)}) %tuple.42), condition=%wide.while_cond.1, body=%wide.while_body.1.sunk | while | flops 2 | bytes 131189 | solution.py:236
  275.8 19.7 %custom-call.18 = f32[2,128,128]{1,2,0:T(8,128)S(1)} custom-call(f32[2,128,128]{2,1,0:T(8,128)S(1)} %get-tuple-element.50), custom_call_target="InvertDiagBlocksLowerTriangular" | custom-call | tf_op jit(solution)/shard_map/triangular_solve | solution.py:236
  (101 shorter events, 39.4 us)
Async XLA Ops:
  20.0 20.2 %collective-permute-start.4 = (f32[512,256]{1,0:T(8,128)}, f32[512,256]{1,0:T(8,128)S(1)}, u32[]{:S(2)}, u32[]{:S(2)}) collective-permute-start(f32[512,256]{1,0:T(8,128)} %get-tuple-element.26), channel_id=1, source_target_pairs={{1,0},{2,1},{3,2},{4,3},{5,4},{6,5},{7,6},{9,8},{10,9},{11,10},{12... | collective-permute-start | bytes 1572872 | tf_op jit(solution)/shard_map/ppermute | solution.py:17
  37.1 14.8 %copy-start.5 = (f32[1,4]{1,0:T(1,128)S(1)}, f32[1,4]{1,0:T(1,128)}, u32[]{:S(2)}) copy-start(f32[1,4]{1,0:T(1,128)} %param.11) | copy-start | bytes 52
  37.1 21.2 %collective-permute-start = (f32[512,256]{1,0:T(8,128)}, f32[512,256]{1,0:T(8,128)S(1)}, u32[]{:S(2)}, u32[]{:S(2)}) collective-permute-start(f32[512,256]{1,0:T(8,128)} %get-tuple-element.20), channel_id=1, source_target_pairs={{1,0},{2,1},{3,2},{4,3},{5,4},{6,5},{7,6},{9,8},{10,9},{11,10},{12... | collective-permute-start | bytes 1572872 | tf_op jit(solution)/shard_map/ppermute | solution.py:17
  40.2 0.8 copy-start.4
  45.7 24.6 %collective-permute-start.5 = (f32[512,256]{1,0:T(8,128)}, f32[512,256]{1,0:T(8,128)S(1)}, u32[]{:S(2)}, u32[]{:S(2)}) collective-permute-start(f32[512,256]{1,0:T(8,128)} %get-tuple-element.27), channel_id=1, source_target_pairs={{0,1},{1,2},{2,3},{3,4},{4,5},{5,6},{6,7},{8,9},{9,10},{10,11},{11... | collective-permute-start | bytes 1572872 | tf_op jit(solution)/shard_map/ppermute | solution.py:17
  58.2 0.8 copy-start.3
  63.7 25.6 %collective-permute-start.1 = (f32[512,256]{1,0:T(8,128)}, f32[512,256]{1,0:T(8,128)S(1)}, u32[]{:S(2)}, u32[]{:S(2)}) collective-permute-start(f32[512,256]{1,0:T(8,128)} %get-tuple-element.21), channel_id=1, source_target_pairs={{0,1},{1,2},{2,3},{3,4},{4,5},{5,6},{6,7},{8,9},{9,10},{10,11},{11... | collective-permute-start | bytes 1572872 | tf_op jit(solution)/shard_map/ppermute | solution.py:17
  70.3 0.8 copy-start.6
  89.3 27.9 %collective-permute-start.6 = (f32[4,512,128]{2,1,0:T(8,128)}, f32[4,512,128]{2,1,0:T(8,128)S(1)}, u32[]{:S(2)}, u32[]{:S(2)}) collective-permute-start(f32[4,512,128]{2,1,0:T(8,128)} %get-tuple-element.30), channel_id=1, source_target_pairs={{0,8},{8,0},{16,24},{24,16},{1,9},{9,1},{17,25},{25,17},{2,10},{10... | collective-permute-start | bytes 3145736 | tf_op jit(solution)/shard_map/ppermute | solution.py:21
  89.3 0.8 copy-start.7
  90.2 28.0 %copy-start = (f32[4,512,128]{2,1,0:T(8,128)S(1)}, f32[4,512,128]{2,1,0:T(8,128)}, u32[]{:S(2)}) copy-start(f32[4,512,128]{2,1,0:T(8,128)} %get-tuple-element.29) | copy-start | bytes 3145732
  116.1 5.5 %copy-start.1 = (f32[4,512,128]{2,1,0:T(8,128)S(1)}, f32[4,512,128]{2,1,0:T(8,128)}, u32[]{:S(2)}) copy-start(f32[4,512,128]{2,1,0:T(8,128)} %get-tuple-element.23) | copy-start | bytes 3145732
  116.1 5.5 %collective-permute-start.2 = (f32[4,512,128]{2,1,0:T(8,128)}, f32[4,512,128]{2,1,0:T(8,128)S(1)}, u32[]{:S(2)}, u32[]{:S(2)}) collective-permute-start(f32[4,512,128]{2,1,0:T(8,128)} %get-tuple-element.24), channel_id=1, source_target_pairs={{0,8},{8,0},{16,24},{24,16},{1,9},{9,1},{17,25},{25,17},{2,10},{10... | collective-permute-start | bytes 3145736 | tf_op jit(solution)/shard_map/ppermute | solution.py:21
  116.7 6.0 %collective-permute-start.10 = (f32[4,512,128]{2,1,0:T(8,128)}, f32[4,512,128]{2,1,0:T(8,128)}, u32[]{:S(2)}, u32[]{:S(2)}) collective-permute-start(f32[4,512,128]{2,1,0:T(8,128)} %get-tuple-element.34), channel_id=1, source_target_pairs={{0,8},{8,0},{16,24},{24,16},{1,9},{9,1},{17,25},{25,17},{2,10},{10... | collective-permute-start | bytes 3145736 | tf_op jit(solution)/shard_map/ppermute | solution.py:21
  116.7 9.6 %collective-permute-start.8 = (f32[4,512,128]{2,1,0:T(8,128)}, f32[4,512,128]{2,1,0:T(8,128)}, u32[]{:S(2)}, u32[]{:S(2)}) collective-permute-start(f32[4,512,128]{2,1,0:T(8,128)} %get-tuple-element.32), channel_id=1, source_target_pairs={{0,8},{8,0},{16,24},{24,16},{1,9},{9,1},{17,25},{25,17},{2,10},{10... | collective-permute-start | bytes 3145736 | tf_op jit(solution)/shard_map/ppermute | solution.py:21
  117.2 1.0 copy-start.2
  119.5 14.9 %collective-permute-start.7 = (f32[2,512,128]{2,1,0:T(8,128)S(1)}, f32[2,512,128]{2,1,0:T(8,128)S(1)}, u32[]{:S(2)}, u32[]{:S(2)}) collective-permute-start(f32[2,512,128]{2,1,0:T(8,128)S(1)} %slice.178), channel_id=1, source_target_pairs={{0,16},{8,24},{16,0},{24,8},{1,17},{9,25},{17,1},{25,9},{2,18},{10... | collective-permute-start | bytes 1572872 | tf_op jit(solution)/shard_map/ppermute | solution.py:21
  122.6 23.2 %collective-permute-start.3 = (f32[2,512,128]{2,1,0:T(8,128)}, f32[2,512,128]{2,1,0:T(8,128)}, u32[]{:S(2)}, u32[]{:S(2)}) collective-permute-start(f32[2,512,128]{2,1,0:T(8,128)} %slice.176), channel_id=1, source_target_pairs={{0,16},{8,24},{16,0},{24,8},{1,17},{9,25},{17,1},{25,9},{2,18},{10... | collective-permute-start | bytes 1572872 | tf_op jit(solution)/shard_map/ppermute | solution.py:21
  124.3 32.6 %collective-permute-start.11 = (f32[2,512,128]{2,1,0:T(8,128)S(1)}, f32[2,512,128]{2,1,0:T(8,128)S(1)}, u32[]{:S(2)}, u32[]{:S(2)}) collective-permute-start(f32[2,512,128]{2,1,0:T(8,128)S(1)} %slice.182), channel_id=1, source_target_pairs={{0,16},{8,24},{16,0},{24,8},{1,17},{9,25},{17,1},{25,9},{2,18},{10... | collective-permute-start | bytes 1572872 | tf_op jit(solution)/shard_map/ppermute | solution.py:21
  128.1 39.4 %collective-permute-start.9 = (f32[2,512,128]{2,1,0:T(8,128)S(1)}, f32[2,512,128]{2,1,0:T(8,128)S(1)}, u32[]{:S(2)}, u32[]{:S(2)}) collective-permute-start(f32[2,512,128]{2,1,0:T(8,128)S(1)} %slice.180), channel_id=1, source_target_pairs={{0,16},{8,24},{16,0},{24,8},{1,17},{9,25},{17,1},{25,9},{2,18},{10... | collective-permute-start | bytes 1572872 | tf_op jit(solution)/shard_map/ppermute | solution.py:21
  169.4 1.6 collective-permute-start.12
  171.2 8.4 %collective-permute-start.13 = (f32[64,512]{0,1:T(8,128)S(1)}, f32[64,512]{0,1:T(8,128)S(1)}, u32[]{:S(2)}, u32[]{:S(2)}) collective-permute-start(f32[64,512]{0,1:T(8,128)S(1)} %constant_dynamic-slice_fusion.2), channel_id=1, source_target_pairs={{0,16},{8,24},{16,0},{24,8},{1,17},{9,25},{17,1},{25,9},{2,18},{10... | collective-permute-start | bytes 393224 | tf_op jit(solution)/shard_map/ppermute | solution.py:21
  179.9 14.7 %collective-permute-start.14 = (f32[32,512]{0,1:T(8,128)S(1)}, f32[32,512]{0,1:T(8,128)S(1)}, u32[]{:S(2)}, u32[]{:S(2)}) collective-permute-start(f32[32,512]{0,1:T(8,128)S(1)} %constant_dynamic-slice_fusion.1), channel_id=1, source_target_pairs={{0,1},{1,0},{2,3},{3,2},{4,5},{5,4},{6,7},{7,6},{8,9},{9,8},{10,11... | collective-permute-start | bytes 196616 | tf_op jit(solution)/shard_map/ppermute | solution.py:21
  194.7 11.1 %collective-permute-start.17 = (f32[32,512]{0,1:T(8,128)S(1)}, f32[32,512]{0,1:T(8,128)S(1)}, u32[]{:S(2)}, u32[]{:S(2)}) collective-permute-start(f32[32,512]{0,1:T(8,128)S(1)} %dynamic-slice_add_fusion), channel_id=1, source_target_pairs={{0,6},{1,7},{2,4},{3,5},{4,2},{5,3},{6,0},{7,1},{8,14},{9,15},{10,... | collective-permute-start | bytes 196616 | tf_op jit(solution)/shard_map/ppermute | solution.py:21
  197.1 22.5 %collective-permute-start.16 = (f32[32,512]{0,1:T(8,128)S(1)}, f32[32,512]{0,1:T(8,128)S(1)}, u32[]{:S(2)}, u32[]{:S(2)}) collective-permute-start(f32[32,512]{0,1:T(8,128)S(1)} %dynamic-slice_add_fusion), channel_id=1, source_target_pairs={{0,4},{1,5},{2,6},{3,7},{4,0},{5,1},{6,2},{7,3},{8,12},{9,13},{10,... | collective-permute-start | bytes 196616 | tf_op jit(solution)/shard_map/ppermute | solution.py:21
  197.8 21.7 %collective-permute-start.15 = (f32[32,512]{0,1:T(8,128)S(1)}, f32[32,512]{0,1:T(8,128)S(1)}, u32[]{:S(2)}, u32[]{:S(2)}) collective-permute-start(f32[32,512]{0,1:T(8,128)S(1)} %dynamic-slice_add_fusion), channel_id=1, source_target_pairs={{0,2},{1,3},{2,0},{3,1},{4,6},{5,7},{6,4},{7,5},{8,10},{9,11},{10,... | collective-permute-start | bytes 196616 | tf_op jit(solution)/shard_map/ppermute | solution.py:21
  219.6 7.5 %collective-permute-start.18 = (f32[32,512]{0,1:T(8,128)S(1)}, f32[32,512]{0,1:T(8,128)S(1)}, u32[]{:S(2)}, u32[]{:S(2)}) collective-permute-start(f32[32,512]{0,1:T(8,128)S(1)} %add_add_fusion), channel_id=1, source_target_pairs={{0,1},{1,0},{2,3},{3,2},{4,5},{5,4},{6,7},{7,6},{8,9},{9,8},{10,11... | collective-permute-start | bytes 196616 | tf_op jit(solution)/shard_map/ppermute | solution.py:21
  227.3 6.7 %collective-permute-start.19 = (f32[64,512]{0,1:T(8,128)S(1)}, f32[64,512]{0,1:T(8,128)S(1)}, u32[]{:S(2)}, u32[]{:S(2)}) collective-permute-start(f32[64,512]{0,1:T(8,128)S(1)} %maximum_select_fusion.1), channel_id=1, source_target_pairs={{0,16},{8,24},{16,0},{24,8},{1,17},{9,25},{17,1},{25,9},{2,18},{10... | collective-permute-start | bytes 393224 | tf_op jit(solution)/shard_map/ppermute | solution.py:21
  234.2 1.6 collective-permute-start.20

commit v2 on v1

v2 whole, which is shorter than its diff:
```python
import functools
import jax
import jax.numpy as jnp
from jax import lax
from jax.experimental import pallas as pl
from jax.experimental.pallas import tpu as pltpu
from jax.sharding import PartitionSpec as P


F32 = jnp.float32
BF16 = jnp.bfloat16
LANES = 128
AHEAD = 3
STEP = 16
HIGHEST = lax.Precision.HIGHEST


def shifted(x, axis, by):
    length = lax.axis_size(axis)
    pairs = [(i, i + by) for i in range(length) if 0 <= i + by < length]
    return lax.ppermute(x, axis, pairs)


def flipped(x, axis, mask):
    return lax.ppermute(x, axis, [(i, i ^ mask) for i in range(lax.axis_size(axis))])


def complex_apply(stacked, vectors):
    order = stacked.shape[0] // 2
    width = vectors.shape[1] // 2
    out = jnp.dot(stacked, vectors.astype(BF16), preferred_element_type=F32)
    real = out[:order, :width] - out[order:, width:]
    imag = out[:order, width:] + out[order:, :width]
    return jnp.concatenate([real, imag], axis=1)


def real_apply(matrix, vectors):
    return jnp.dot(matrix, vectors.astype(BF16), preferred_element_type=F32)


def transposed_apply(matrix, vectors):
    return lax.dot_general(
        matrix, vectors.astype(BF16), (((0,), (0,)), ((), ())), preferred_element_type=F32
    )


def block_copies(k, f_hbm, g_hbm, u_hbm, fv, gv, uv, sem):
    return (
        pltpu.make_async_copy(f_hbm.at[k], fv.at[k], sem.at[0, k]),
        pltpu.make_async_copy(g_hbm.at[k], gv.at[k], sem.at[1, k]),
        pltpu.make_async_copy(u_hbm.at[k], uv.at[k], sem.at[2, k]),
    )


def fetch_ahead(blocks, copies, k):
    @pl.when(k + AHEAD < blocks)
    def _():
        for copy in copies(k + AHEAD):
            copy.start()


def first_kernel(groups, f_hbm, g_hbm, u_hbm, i_hbm, *refs):
    tops, sbs = refs[:groups], refs[groups : 2 * groups]
    fv, gv, uv, sv, ut, hold, sem, s_sem = refs[2 * groups :]
    blocks = gv.shape[0]
    order = uv.shape[1]
    width = fv.shape[2] // groups
    lanes = [slice(c * width, (c + 1) * width) for c in range(groups)]
    copies = functools.partial(
        block_copies, f_hbm=f_hbm, g_hbm=g_hbm, u_hbm=u_hbm, fv=fv, gv=gv, uv=uv, sem=sem
    )
    fetch = functools.partial(fetch_ahead, blocks, copies)
    for k in range(min(AHEAD, blocks)):
        for copy in copies(k):
            copy.start()
    s_copy = pltpu.make_async_copy(i_hbm.at[0], sv, s_sem)
    for copy in copies(0):
        copy.wait()
    for c in range(groups):
        out = jnp.dot(gv[0], fv[0, :, lanes[c]], preferred_element_type=F32)
        hold[c, 0] = jnp.concatenate([out[:order], out[order:]], axis=1)
    ut[0] = uv[0].T

    fetch(0)

    def forward(k, carry):
        fetch(k)
        for copy in copies(k):
            copy.wait()
        coupled = [real_apply(ut[(k + 1) % 2], hold[c, k - 1]) for c in range(groups)]
        for c in range(groups):
            given = fv[k, :, lanes[c]].astype(F32)
            hold[c, k] = complex_apply(
                gv[k], coupled[c] + jnp.concatenate([given, jnp.zeros_like(given)], axis=1)
            )
        ut[k % 2] = uv[k].T
        return carry

    s_copy.start()
    lax.fori_loop(1, blocks, forward, 0)
    s_copy.wait()
    for c in range(groups):
        sbs[c][...] = complex_apply(sv[...], hold[c, blocks - 1])

    def backward(i, carry):
        k = blocks - 2 - i
        coupled = [real_apply(uv[k], hold[c, k + 1]) for c in range(groups)]
        for c in range(groups):
            hold[c, k] = hold[c, k] + complex_apply(gv[k], coupled[c])
        return carry

    lax.fori_loop(0, blocks - 1, backward, 0)
    for c in range(groups):
        tops[c][...] = hold[c, 0]


def first_solve(groups, source, inverse, coupled, factors):
    blocks, stacked, order = inverse.shape
    vectors = source.shape[2]
    width = vectors // groups
    tip = jax.ShapeDtypeStruct((order, 2 * width), F32)
    hbm = pl.BlockSpec(memory_space=pl.ANY)
    vmem = pl.BlockSpec(memory_space=pltpu.VMEM)
    flops = 2 * order * order * 2 * vectors * (5 * blocks - 3)
    outs = pl.pallas_call(
        functools.partial(first_kernel, groups),
        out_shape=(tip,) * (2 * groups),
        in_specs=[hbm] * 4,
        out_specs=(vmem,) * (2 * groups),
        scratch_shapes=[
            pltpu.VMEM((blocks, order, vectors), BF16),
            pltpu.VMEM((blocks, stacked, order), BF16),
            pltpu.VMEM((blocks, order, order), BF16),
            pltpu.VMEM((stacked, order), BF16),
            pltpu.VMEM((2, order, order), BF16),
            pltpu.VMEM((groups, blocks, order, 2 * width), F32),
            pltpu.SemaphoreType.DMA((3, blocks)),
            pltpu.SemaphoreType.DMA,
        ],
        cost_estimate=pl.CostEstimate(flops=flops, transcendentals=0, bytes_accessed=14 * 2**20),
        name="first_solve",
    )(source, inverse, coupled, factors)
    return outs[:groups], outs[groups:]


def below_kernel(sb_hbm, next_hbm, i_hbm, u_hbm, below_ref, lifted_ref, sb, top_next, kv, uv, sem):
    copies = (
        pltpu.make_async_copy(next_hbm, top_next, sem.at[0]),
        pltpu.make_async_copy(i_hbm.at[1], kv, sem.at[1]),
        pltpu.make_async_copy(sb_hbm, sb, sem.at[2]),
        pltpu.make_async_copy(u_hbm.at[u_hbm.shape[0] - 1], uv, sem.at[3]),
    )
    for copy in copies:
        copy.start()
    copies[0].wait()
    copies[1].wait()
    product = complex_apply(kv[...], top_next[...])
    copies[2].wait()
    below = sb[...] - product
    below_ref[...] = below
    copies[3].wait()
    lifted_ref[...] = transposed_apply(uv[...], below)


def interface_below(s_times, top_next, factors, coupled):
    shape = jax.ShapeDtypeStruct(top_next.shape, F32)
    order, width = top_next.shape
    vmem = pl.BlockSpec(memory_space=pltpu.VMEM)
    hbm = pl.BlockSpec(memory_space=pl.ANY)
    return pl.pallas_call(
        below_kernel,
        out_shape=(shape, shape),
        in_specs=[hbm] * 4,
        out_specs=(vmem, vmem),
        scratch_shapes=[
            pltpu.VMEM(top_next.shape, F32),
            pltpu.VMEM(top_next.shape, F32),
            pltpu.VMEM((2 * order, order), BF16),
            pltpu.VMEM((order, order), BF16),
            pltpu.SemaphoreType.DMA((4,)),
        ],
        cost_estimate=pl.CostEstimate(
            flops=6 * order * order * width, transcendentals=0, bytes_accessed=4 * 2**20
        ),
        name="interface_below",
    )(s_times, top_next, factors, coupled)


def above_kernel(last_ref, below_ref, next_ref, i_hbm, u_hbm, added_ref, wv, uv, sem):
    copies = (
        pltpu.make_async_copy(i_hbm.at[2], wv, sem.at[0]),
        pltpu.make_async_copy(u_hbm.at[u_hbm.shape[0] - 1], uv, sem.at[1]),
    )
    for copy in copies:
        copy.start()
    copies[0].wait()
    above = next_ref[...] - complex_apply(wv[...], below_ref[...])
    above = jnp.where(last_ref[0] == 1, jnp.zeros_like(above), above)
    copies[1].wait()
    added_ref[...] = real_apply(uv[...], above)


def interface_above(topmost, below, top_next, factors, coupled):
    order, width = top_next.shape
    vmem = pl.BlockSpec(memory_space=pltpu.VMEM)
    hbm = pl.BlockSpec(memory_space=pl.ANY)
    return pl.pallas_call(
        above_kernel,
        out_shape=jax.ShapeDtypeStruct(top_next.shape, F32),
        in_specs=[pl.BlockSpec(memory_space=pltpu.SMEM), vmem, vmem, hbm, hbm],
        out_specs=vmem,
        scratch_shapes=[
            pltpu.VMEM((2 * order, order), BF16),
            pltpu.VMEM((order, order), BF16),
            pltpu.SemaphoreType.DMA((2,)),
        ],
        cost_estimate=pl.CostEstimate(
            flops=6 * order * order * width, transcendentals=0, bytes_accessed=4 * 2**20
        ),
        name="interface_above",
    )(topmost, below, top_next, factors, coupled)


def second_kernel(
    lane, owners, place_ref, scale_ref, f_hbm, g_hbm, u_hbm, arrive_hbm, added_hbm,
    keep_y, keep_z, send_y, send_z, fv, gv, uv, ut, hold, yv, zv, arrive, added, sem, out_sem, tip_sem,
):
    blocks = gv.shape[0]
    count = blocks // owners
    width = fv.shape[2]
    copies = functools.partial(
        block_copies, f_hbm=f_hbm.at[:, :, pl.ds(lane, width)], g_hbm=g_hbm, u_hbm=u_hbm,
        fv=fv, gv=gv, uv=uv, sem=sem,
    )
    fetch = functools.partial(fetch_ahead, blocks, copies)
    for k in range(min(AHEAD, blocks)):
        for copy in copies(k):
            copy.start()

    arrive_copy = pltpu.make_async_copy(arrive_hbm, arrive, tip_sem.at[0])
    added_copy = pltpu.make_async_copy(added_hbm, added, tip_sem.at[1])
    arrive_copy.start()

    def given(k):
        real = fv[k].astype(F32)
        return jnp.concatenate([real, jnp.zeros_like(real)], axis=1)

    for copy in copies(0):
        copy.wait()
    arrive_copy.wait()
    hold[0] = complex_apply(gv[0], given(0) + arrive[...])
    added_copy.start()
    ut[0] = uv[0].T

    fetch(0)

    def forward(k, carry):
        fetch(k)
        for copy in copies(k):
            copy.wait()
        coupled = real_apply(ut[(k + 1) % 2], hold[k - 1])
        hold[k] = complex_apply(gv[k], given(k) + coupled)
        ut[k % 2] = uv[k].T
        return carry

    lax.fori_loop(1, blocks - 1, forward, 0)
    last = blocks - 1
    for copy in copies(last):
        copy.wait()
    added_copy.wait()
    coupled = real_apply(ut[(last + 1) % 2], hold[last - 1])
    hold[last] = complex_apply(gv[last], (given(last) + added[...]) + coupled)

    wr, wi, zwr, zwi = scale_ref[0], scale_ref[1], scale_ref[2], scale_ref[3]
    low = place_ref[0]
    high = place_ref[1]

    def emit(k, x):
        real, imag = x[:, :width], x[:, width:]
        y = wr * real - wi * imag
        z = zwr * real - zwi * imag - wr * fv[k].astype(F32)
        owner = k // count
        slot = ((owner // 2) ^ high) * count + k % count

        yv[k] = y
        zv[k] = z

        @pl.when(owner % 2 == low)
        def _():
            pltpu.make_async_copy(yv.at[k], keep_y.at[slot], out_sem.at[0, k]).start()
            pltpu.make_async_copy(zv.at[k], keep_z.at[slot], out_sem.at[1, k]).start()

        @pl.when(owner % 2 != low)
        def _():
            pltpu.make_async_copy(yv.at[k], send_y.at[slot], out_sem.at[0, k]).start()
            pltpu.make_async_copy(zv.at[k], send_z.at[slot], out_sem.at[1, k]).start()

    emit(last, hold[last])

    def backward(i, carry):
        k = blocks - 2 - i
        x = hold[k] + complex_apply(gv[k], real_apply(uv[k], hold[k + 1]))
        hold[k] = x
        emit(k, x)
        return carry

    lax.fori_loop(0, blocks - 1, backward, 0)
    for k in range(blocks):
        pltpu.make_async_copy(yv.at[k], keep_y.at[0], out_sem.at[0, k]).wait()
        pltpu.make_async_copy(zv.at[k], keep_z.at[0], out_sem.at[1, k]).wait()


def second_solve(chunk, width, owners, place, scales, source, inverse, coupled, arriving, added):
    blocks, stacked, order = inverse.shape
    part = jax.ShapeDtypeStruct((blocks // 2, order, width), F32)
    hbm = pl.BlockSpec(memory_space=pl.ANY)
    vmem = pl.BlockSpec(memory_space=pltpu.VMEM)
    smem = pl.BlockSpec(memory_space=pltpu.SMEM)
    flops = 2 * order * order * 2 * width * (5 * blocks - 3)
    return pl.pallas_call(
        functools.partial(second_kernel, chunk * width, owners),
        out_shape=(part,) * 4,
        in_specs=[smem, smem] + [hbm] * 5,
        out_specs=(hbm,) * 4,
        scratch_shapes=[
            pltpu.VMEM((blocks, order, width), BF16),
            pltpu.VMEM((blocks, stacked, order), BF16),
            pltpu.VMEM((blocks, order, order), BF16),
            pltpu.VMEM((2, order, order), BF16),
            pltpu.VMEM((blocks, order, 2 * width), F32),
            pltpu.VMEM((blocks, order, width), F32),
            pltpu.VMEM((blocks, order, width), F32),
            pltpu.VMEM((order, 2 * width), F32),
            pltpu.VMEM((order, 2 * width), F32),
            pltpu.SemaphoreType.DMA((3, blocks)),
            pltpu.SemaphoreType.DMA((2, blocks)),
            pltpu.SemaphoreType.DMA((2,)),
        ],
        cost_estimate=pl.CostEstimate(flops=flops, transcendentals=0, bytes_accessed=16 * 2**20),
        name="second_solve",
    )(place, scales, source, inverse, coupled, arriving, added)


def factor_kernel(total, gram_ref, y_ref, basis_ref, inverse_ref, acc):
    n = gram_ref.shape[0]
    rows = lax.broadcasted_iota(jnp.int32, (n, n), 0)
    cols = lax.broadcasted_iota(jnp.int32, (n, n), 1)
    acc[:, :n] = gram_ref[...] / total
    acc[:, n:] = (rows == cols).astype(F32)
    lane = 128
    row = lax.broadcasted_iota(jnp.int32, (STEP, lane), 0)
    for r in range(0, n, STEP):
        low = r // lane * lane
        high = (r + STEP + lane - 1) // lane * lane
        panel = acc[r : r + STEP, low : n + high]
        tiles = [panel[:, i:i+lane] for i in range(0, panel.shape[1], lane)]
        cols_ = [jnp.broadcast_to(panel[:, r-low+j:r-low+j+1], (STEP, lane)) for j in range(STEP)]
        scale = jnp.ones((STEP, lane), F32)
        for k in range(STEP):
            inv = lax.rsqrt(jnp.broadcast_to(cols_[k][k:k+1], (STEP, lane)))
            scale = jnp.where(row == k, inv, scale)
            m = jnp.where(row > k, cols_[k], 0.0) * (inv * inv)
            for j in range(k + 1, STEP):
                cols_[j] = cols_[j] - m * jnp.broadcast_to(cols_[j][k:k+1], (STEP, lane))
            tiles = [t - m * jnp.broadcast_to(t[k:k+1], (STEP, lane)) for t in tiles]
        done = jnp.concatenate([t * scale for t in tiles], axis=1)
        acc[r : r + STEP, low : n + high] = done
        if r + STEP < n:
            left = done[:, :n-low].T[r+STEP-low:]
            acc[r+STEP:, low : n + high] -= jnp.dot(left, done, precision=HIGHEST, preferred_element_type=F32)
    inverse = jnp.where(cols <= rows, acc[:, n:], 0.0)
    nt = (((1,), (1,)), ((), ()))
    basis_ref[...] = lax.dot_general(y_ref[...], inverse, nt, precision=HIGHEST, preferred_element_type=F32)
    inverse_ref[...] = inverse


def congruence_kernel(total, inverse_ref, proj_ref, ray_ref):
    inverse = inverse_ref[...]
    middle = jnp.dot(
        inverse, proj_ref[...] / total, precision=HIGHEST, preferred_element_type=F32
    )
    ray_ref[...] = lax.dot_general(
        middle, inverse, (((1,), (1,)), ((), ())), precision=HIGHEST, preferred_element_type=F32
    )


def congruence(total, inverse, projected):
    vmem = pl.BlockSpec(memory_space=pltpu.VMEM)
    return pl.pallas_call(
        functools.partial(congruence_kernel, float(total)),
        out_shape=jax.ShapeDtypeStruct(inverse.shape, F32),
        in_specs=[vmem] * 2,
        out_specs=vmem,
        cost_estimate=pl.CostEstimate(flops=2**30, transcendentals=0, bytes_accessed=2**20),
        name="congruence",
    )(inverse, projected)


def orthonormalized(total, gram, y):
    n = gram.shape[0]
    vmem = pl.BlockSpec(memory_space=pltpu.VMEM)
    return pl.pallas_call(
        functools.partial(factor_kernel, float(total)),
        out_shape=(jax.ShapeDtypeStruct(y.shape, F32), jax.ShapeDtypeStruct((n, n), F32)),
        in_specs=[vmem] * 2,
        out_specs=(vmem, vmem),
        scratch_shapes=[pltpu.VMEM((n, 2 * n), F32)],
        cost_estimate=pl.CostEstimate(
            flops=12 * 2**30, transcendentals=0, bytes_accessed=3 * 2**20
        ),
        name="orthonormalized",
    )(gram, y)


def inner_products(left, right_side):
    return lax.dot_general(
        left,
        right_side,
        (((0,), (0,)), ((), ())),
        precision=lax.Precision.HIGHEST,
        preferred_element_type=F32,
    )


def summed_everywhere(x, steps, far):
    kept = []
    for axis, mask in steps:
        half = x.shape[0] // 2
        bit = (lax.axis_index(axis) // mask) % 2
        mine = lax.dynamic_slice_in_dim(x, bit * half, half, 0)
        other = lax.dynamic_slice_in_dim(x, (1 - bit) * half, half, 0)
        x = mine + flipped(other, axis, mask)
        kept.append(bit)
    axis, masks = far
    x = x + sum(flipped(x, axis, mask) for mask in masks)
    for (axis, mask), bit in zip(reversed(steps), reversed(kept)):
        other = flipped(x, axis, mask)
        x = jnp.where(bit == 0, jnp.concatenate([x, other]), jnp.concatenate([other, x]))
    return x


def on_device(initial_block, coupling, pivots, interface, pole_values):
    blocks = coupling.shape[1]
    order = coupling.shape[2]
    vectors = initial_block.shape[3]
    width = min(LANES, vectors)
    owners = lax.axis_size("pole")
    parts = lax.axis_size("dom")
    count = blocks // owners
    source = initial_block[0]
    coupled = coupling[0]
    inverse = pivots[0, 0].reshape(blocks, 2 * order, order)
    factors = interface[0, 0].reshape(3, 2 * order, order)
    pole = lax.axis_index("pole")
    dom = lax.axis_index("dom")
    topmost = (dom == parts - 1).astype(jnp.int32).reshape(1)
    place = jnp.stack([pole % 2, pole // 2]).astype(jnp.int32)
    real_z, imag_z, real_w, imag_w = (pole_values[0, i] for i in range(4))
    scales = jnp.stack(
        [real_w, imag_w, real_w * real_z - imag_w * imag_z, real_w * imag_z + imag_w * real_z]
    )
    chunks = vectors // width
    tips, s_times = first_solve(chunks, source, inverse, coupled, factors)
    tops, belows, arrivals, added = [], [], [], []
    for c in range(chunks):
        tops.append(shifted(tips[c], "dom", -1))
    for c in range(chunks):
        belows.append(interface_below(s_times[c], tops[c], factors, coupled))
        arrivals.append(shifted(belows[c][1], "dom", 1))
        added.append(interface_above(topmost, belows[c][0], tops[c], factors, coupled))
    masks = [1 << i for i in range(1, owners.bit_length() - 1)]

    def pole_sum(keep, send):
        other = flipped(send, "pole", 1)
        terms = [keep, other]
        for mask in masks:
            half = terms[0].shape[0] // 2
            out = sum(term[half:] for term in terms)
            terms = [term[:half] for term in terms] + [flipped(out, "pole", mask)]
        return sum(terms).reshape(count * order, width)

    own_y, own_z = [], []
    for c in range(chunks):
        keep_y, keep_z, send_y, send_z = second_solve(
            c, width, owners, place, scales, source, inverse, coupled, arrivals[c], added[c]
        )
        own_y.append(pole_sum(keep_y, send_y))
        own_z.append(pole_sum(keep_z, send_z))
    own_y = jnp.concatenate(own_y, axis=1)
    own_z = jnp.concatenate(own_z, axis=1)
    near = [("pole", 1 << i) for i in range(owners.bit_length() - 1)] + [("dom", 1)]
    far = ("dom", tuple(range(2, parts, 2)))
    gram = summed_everywhere(inner_products(own_y, own_y), near, far)
    projected = summed_everywhere(inner_products(own_y, own_z), near, far)
    row_total = blocks * order * parts
    basis, inverse_factor = orthonormalized(row_total, gram, own_y)
    rayleigh = congruence(row_total, inverse_factor, projected)
    return (basis.reshape(1, count, order, vectors), rayleigh)


def solution(mesh):
    in_specs = (
        P("dom", None, None, None),
        P("dom", None, None, None),
        P("pole", "dom", None, None, None, None),
        P("pole", "dom", None, None, None, None),
        P("pole", None),
    )
    out_specs = (P("dom", "pole", None, None), P())
    return jax.shard_map(
        on_device, mesh=mesh, in_specs=in_specs, out_specs=out_specs, check_vma=False
    )
```

time: 308 us -> 213 us (0.69); the launches traced: 303 us -> 212 us
  other arithmetic: 63.3 us -> 12.5 us
  waiting for transfers between devices: 83 us -> 57.1 us
  local copies, waits for them, and re-layouts: 17.8 us -> 4.03 us
  starting transfers between devices: 37.4 us -> 42.9 us
  matrix products: 8.38 us -> 3.66 us
    another operation x9 -> x0, other arithmetic: 53.8 us -> none  [the longest x6 34.1 us: on_device(): factor = jnp.linalg.cholesky(gram)]
    ppermute x17 -> x26, waiting for transfers between devices: 83 us -> 41.8 us  [flipped(): lax.ppermute(x, axis, [(i, i ^ mask) for i in range(lax.axis_size(axis))])]
    ppermute x4, waiting for transfers between devices: 0.01 us -> 15.3 us  [shifted(): return lax.ppermute(x, axis, pairs)]
    pallas_call x4 -> x7, Pallas kernels: 40.9 us -> 50.8 us  [the longest x1 19.1 us: first_solve(): pl.pallas_call(functools.partial(first_kernel, groups), out_shape=(tip,)...]
    pallas_call x2, Pallas kernels: 44 us -> 34.8 us  [second_solve(): pl.pallas_call(functools.partial(second_kernel, chunk * width, owners), o...]
    ppermute x17 -> x26, starting transfers between devices: 23.8 us -> 32.9 us  [flipped(): lax.ppermute(x, axis, [(i, i ^ mask) for i in range(lax.axis_size(axis))])]
    another operation x11 -> x0, matrix products: 4.76 us -> none  [the longest x9 4.29 us: lower_solve(): lax.linalg.triangular_solve(factor, right_side, left_side=True, lower=True)]
    slice x5 -> x0, local copies, waits for them, and re-layouts: 4.53 us -> none  [the longest x1 3.59 us: on_device(): factors[2]]
  transfers between devices with their start and end apart: 21 -> 30, of which waited for: 12 -> 9; matrix products, arithmetic and copies ran while one was open for 5% -> 8% of each run, Pallas kernels for 23% -> 30%
where the time goes in v2:
time: 213 us; the launch traced here: 212 us
  Pallas kernels  85.6 us (40%)
  waiting for transfers between devices  57.1 us (27%)
  starting transfers between devices  42.9 us (20%)
  other arithmetic  12.5 us (6%)
  between operations  6.08 us (3%)
  local copies, waits for them, and re-layouts  4.03 us (2%)
  matrix products  3.66 us (2%)
    ppermute x26, waiting for transfers between devices, flipped(): lax.ppermute(x, axis, [(i, i ^ mask) for i in range(lax.axis_size(axis))])  41.8 us
    pallas_call x2, Pallas kernels, second_solve(): pl.pallas_call(functools.partial(second_kernel, chunk * width, owners), o...  34.8 us
    ppermute x26, starting transfers between devices, flipped(): lax.ppermute(x, axis, [(i, i ^ mask) for i in range(lax.axis_size(axis))])  32.9 us
    pallas_call x1, Pallas kernels, first_solve(): pl.pallas_call(functools.partial(first_kernel, groups), out_shape=(tip,)...  19.1 us
    ppermute x4, waiting for transfers between devices, shifted(): return lax.ppermute(x, axis, pairs)  15.3 us
    pallas_call x1, Pallas kernels, orthonormalized(): pl.pallas_call(functools.partial(factor_kernel, float(total)), out_shape=...  13.9 us
    ppermute x4, starting transfers between devices, shifted(): return lax.ppermute(x, axis, pairs)  9.99 us
    pallas_call x2, Pallas kernels, interface_above(): pl.pallas_call(above_kernel, out_shape=jax.ShapeDtypeStruct(top_next.shap...  8.47 us
  transfers between devices with their start and end apart: 30, of which 9 were waited for; matrix products, arithmetic and copies ran while one was open for 8% of the time, Pallas kernels for 30%

profile of v2, /device:TPU:0, one launch (start us, length us, event | category | flops | bytes accessed | tf_op | source)
XLA Modules:
  0.0 211.9 jit_solution(7220404875951426740)
XLA Ops:
  0.6 19.1 %first_solve.1 = (f32[512,256]{1,0:T(8,128)}, f32[512,256]{1,0:T(8,128)}, f32[512,256]{1,0:T(8,128)}, f32[512,256]{1,0:T(8,128)}) custom-call(bf16[8,512,256]{2,1,0:T(8,128)(2,1)} %bitcast.39, bf16[8,1024,512]{2,1,0:T(8,128)(2,1)} %bitcast.36, bf16[8,512,512]{2,1,0:T(8,128)(2,1)} %bitcast.16, bf16[3,1024,512]{2,1,0:T(8,128)(2,1)} %bitcast.23), custom_call_target="tpu_custom_call" | custom-call | flops 9932111872 | bytes 14680064 | tf_op jit(solution)/shard_map/first_solve/pallas_call | solution.py:125
  22.3 15.3 %collective-permute-done.4.next_hbm.next_ref = f32[512,256]{1,0:T(8,128)S(1)} collective-permute-done((f32[512,256]{1,0:T(8,128)}, f32[512,256]{1,0:T(8,128)S(1)}, u32[]{:S(2)}, u32[]{:S(2)}) %collective-permute-start.4) | collective-permute-done | bytes 524320 | tf_op jit(solution)/shard_map/ppermute | solution.py:21
  38.4 3.3 %interface_below.3 = (f32[512,256]{1,0:T(8,128)}, f32[512,256]{1,0:T(8,128)}) custom-call(f32[512,256]{1,0:T(8,128)} %get-tuple-element.26.sb_hbm, f32[512,256]{1,0:T(8,128)} %copy-done.1, bf16[3,1024,512]{2,1,0:T(8,128)(2,1)} %bitcast.24, bf16[8,512,512]{2,1,0:T(8,128)(2,1)} %bitcast.17), custom_call_target="tpu_custom_call" | custom-call | flops 402653184 | bytes 4194304 | tf_op jit(solution)/shard_map/interface_below/pallas_call | solution.py:170
  41.7 4.8 %collective-permute-start.5 = (f32[512,256]{1,0:T(8,128)}, f32[512,256]{1,0:T(8,128)S(1)}, u32[]{:S(2)}, u32[]{:S(2)}) collective-permute-start(f32[512,256]{1,0:T(8,128)} %get-tuple-element.28), channel_id=1, source_target_pairs={{0,1},{1,2},{2,3},{3,4},{4,5},{5,6},{6,7},{8,9},{9,10},{10,11},{11... | collective-permute-start | bytes 1572872 | tf_op jit(solution)/shard_map/ppermute | solution.py:21
  53.0 2.0 pad_maximum_fusion.1.scale_ref
  55.8 3.3 %interface_below.2 = (f32[512,256]{1,0:T(8,128)}, f32[512,256]{1,0:T(8,128)}) custom-call(f32[512,256]{1,0:T(8,128)} %get-tuple-element.20.sb_hbm, f32[512,256]{1,0:T(8,128)} %copy-done, bf16[3,1024,512]{2,1,0:T(8,128)(2,1)} %bitcast.25, bf16[8,512,512]{2,1,0:T(8,128)(2,1)} %bitcast.18), custom_call_target="tpu_custom_call" | custom-call | flops 402653184 | bytes 4194304 | tf_op jit(solution)/shard_map/interface_below/pallas_call | solution.py:170
  59.1 2.6 %collective-permute-start.1 = (f32[512,256]{1,0:T(8,128)}, f32[512,256]{1,0:T(8,128)S(1)}, u32[]{:S(2)}, u32[]{:S(2)}) collective-permute-start(f32[512,256]{1,0:T(8,128)} %get-tuple-element.22), channel_id=1, source_target_pairs={{0,1},{1,2},{2,3},{3,4},{4,5},{5,6},{6,7},{8,9},{9,10},{10,11},{11... | collective-permute-start | bytes 1572872 | tf_op jit(solution)/shard_map/ppermute | solution.py:21
  61.6 4.2 %interface_above.3.added_hbm = f32[512,256]{1,0:T(8,128)} custom-call(s32[1]{0:T(128)} %bitcast.10.last_ref, f32[512,256]{1,0:T(8,128)} %get-tuple-element.29.below_ref, f32[512,256]{1,0:T(8,128)} %copy-done.1, bf16[3,1024,512]{2,1,0:T(8,128)(2,1)} %bitcast.26, bf16[8,512,512]{2,1,0:T(8,128)(2,1)} %bitcast.19), custom_call_target="tpu_custom_call" | custom-call | flops 402653184 | bytes 4194304 | tf_op jit(solution)/shard_map/interface_above/pallas_call | solution.py:207
  66.7 17.4 %second_solve.3 = (f32[4,512,128]{2,1,0:T(8,128)}, f32[4,512,128]{2,1,0:T(8,128)}, f32[4,512,128]{2,1,0:T(8,128)}, f32[4,512,128]{2,1,0:T(8,128)}) custom-call(s32[2]{0:T(128)} %pad_add_fusion.place_ref, f32[4]{0:T(128)} %pad_maximum_fusion.1.scale_ref, bf16[8,512,256]{2,1,0:T(8,128)(2,1)} %bitcast.40, bf16[8,1024,512]{2,1,0:T(8,128)(2,1)} %bitcast.37, ...), custom_call_target="tpu_custom_call" | custom-call | flops 4966055936 | bytes 16777216 | tf_op jit(solution)/shard_map/second_solve/pallas_call | solution.py:320
  84.2 4.3 %interface_above.2.added_hbm = f32[512,256]{1,0:T(8,128)} custom-call(s32[1]{0:T(128)} %bitcast.10.last_ref, f32[512,256]{1,0:T(8,128)} %get-tuple-element.23.below_ref, f32[512,256]{1,0:T(8,128)} %copy-done, bf16[3,1024,512]{2,1,0:T(8,128)(2,1)} %bitcast.27, bf16[8,512,512]{2,1,0:T(8,128)(2,1)} %bitcast.21), custom_call_target="tpu_custom_call" | custom-call | flops 402653184 | bytes 4194304 | tf_op jit(solution)/shard_map/interface_above/pallas_call | solution.py:207
  89.8 17.4 %second_solve.2 = (f32[4,512,128]{2,1,0:T(8,128)}, f32[4,512,128]{2,1,0:T(8,128)}, f32[4,512,128]{2,1,0:T(8,128)}, f32[4,512,128]{2,1,0:T(8,128)}) custom-call(s32[2]{0:T(128)} %pad_add_fusion.place_ref, f32[4]{0:T(128)} %pad_maximum_fusion.1.scale_ref, bf16[8,512,256]{2,1,0:T(8,128)(2,1)} %bitcast.41, bf16[8,1024,512]{2,1,0:T(8,128)(2,1)} %bitcast.38, ...), custom_call_target="tpu_custom_call" | custom-call | flops 4966055936 | bytes 16777216 | tf_op jit(solution)/shard_map/second_solve/pallas_call | solution.py:320
  107.8 1.4 slice_add_fusion.4
  109.2 1.6 collective-permute-start.7
  112.7 1.6 collective-permute-start.3
  116.0 8.1 %collective-permute-done.7 = f32[2,512,128]{2,1,0:T(8,128)S(1)} collective-permute-done((f32[2,512,128]{2,1,0:T(8,128)S(1)}, f32[2,512,128]{2,1,0:T(8,128)S(1)}, u32[]{:S(2)}, u32[]{:S(2)}) %collective-permute-start.7) | collective-permute-done | bytes 524320 | tf_op jit(solution)/shard_map/ppermute | solution.py:25
  125.2 21.4 %collective-permute-done.3 = f32[2,512,128]{2,1,0:T(8,128)S(1)} collective-permute-done((f32[2,512,128]{2,1,0:T(8,128)S(1)}, f32[2,512,128]{2,1,0:T(8,128)S(1)}, u32[]{:S(2)}, u32[]{:S(2)}) %collective-permute-start.3) | collective-permute-done | bytes 524320 | tf_op jit(solution)/shard_map/ppermute | solution.py:25
  147.7 1.8 fusion.9
  149.7 7.2 %collective-permute-done.18 = f32[2,512,128]{2,1,0:T(8,128)S(1)} collective-permute-done((f32[2,512,128]{2,1,0:T(8,128)S(1)}, f32[2,512,128]{2,1,0:T(8,128)S(1)}, u32[]{:S(2)}, u32[]{:S(2)}) %collective-permute-start.18) | collective-permute-done | bytes 524320 | tf_op jit(solution)/shard_map/ppermute | solution.py:25
  158.0 1.8 fusion
  160.0 1.6 collective-permute-start.9
  162.9 1.7 collective-permute-done.9
  164.7 6.9 %collective-permute-start.10 = (f32[32,256]{1,0:T(8,128)S(1)}, f32[32,256]{1,0:T(8,128)S(1)}, u32[]{:S(2)}, u32[]{:S(2)}) collective-permute-start(f32[32,256]{1,0:T(8,128)S(1)} %constant_dynamic-slice_fusion.3), channel_id=1, source_target_pairs={{0,1},{1,0},{2,3},{3,2},{4,5},{5,4},{6,7},{7,6},{8,9},{9,8},{10,11... | collective-permute-start | bytes 98312 | tf_op jit(solution)/shard_map/ppermute | solution.py:25
  171.6 1.3 collective-permute-start.23
  173.5 2.6 %collective-permute-start.13 = (f32[32,256]{1,0:T(8,128)S(1)}, f32[32,256]{1,0:T(8,128)S(1)}, u32[]{:S(2)}, u32[]{:S(2)}) collective-permute-start(f32[32,256]{1,0:T(8,128)S(1)} %dynamic-slice_add_fusion.5), channel_id=1, source_target_pairs={{0,6},{1,7},{2,4},{3,5},{4,2},{5,3},{6,0},{7,1},{8,14},{9,15},{10,... | collective-permute-start | bytes 98312 | tf_op jit(solution)/shard_map/ppermute | solution.py:25
  176.5 1.4 collective-permute-start.11
  177.9 2.7 %collective-permute-start.26 = (f32[32,256]{1,0:T(8,128)S(1)}, f32[32,256]{1,0:T(8,128)S(1)}, u32[]{:S(2)}, u32[]{:S(2)}) collective-permute-start(f32[32,256]{1,0:T(8,128)S(1)} %dynamic-slice_add_fusion.4), channel_id=1, source_target_pairs={{0,6},{1,7},{2,4},{3,5},{4,2},{5,3},{6,0},{7,1},{8,14},{9,15},{10,... | collective-permute-start | bytes 98312 | tf_op jit(solution)/shard_map/ppermute | solution.py:25
  180.5 1.8 collective-permute-start.24
  182.3 2.1 collective-permute-start.14
  186.4 2.1 collective-permute-start.15
  189.3 2.0 collective-permute-start.28
  194.5 13.9 %orthonormalized.1 = (f32[1024,256]{1,0:T(8,128)}, f32[256,256]{1,0:T(8,128)}) custom-call(f32[256,256]{1,0:T(8,128)} %maximum_select_fusion.gram_ref, f32[1024,256]{1,0:T(8,128)} %pad_maximum_fusion.y_ref), custom_call_target="tpu_custom_call" | custom-call | flops 12884901888 | bytes 3145728 | tf_op jit(solution)/shard_map/orthonormalized/pallas_call | solution.py:402
  209.2 2.7 %congruence.1 = f32[256,256]{1,0:T(8,128)} custom-call(f32[256,256]{1,0:T(8,128)} %get-tuple-element.33.inverse_ref, f32[256,256]{1,0:T(8,128)} %maximum_select_fusion.1.proj_ref), custom_call_target="tpu_custom_call" | custom-call | flops 1073741824 | bytes 1048576 | tf_op jit(solution)/shard_map/congruence/pallas_call | solution.py:389
  (89 shorter events, 24.6 us)
Async XLA Ops:
  19.7 17.9 %collective-permute-start.4 = (f32[512,256]{1,0:T(8,128)}, f32[512,256]{1,0:T(8,128)S(1)}, u32[]{:S(2)}, u32[]{:S(2)}) collective-permute-start(f32[512,256]{1,0:T(8,128)} %get-tuple-element.27), channel_id=1, source_target_pairs={{1,0},{2,1},{3,2},{4,3},{5,4},{6,5},{7,6},{9,8},{10,9},{11,10},{12... | collective-permute-start | bytes 1572872 | tf_op jit(solution)/shard_map/ppermute | solution.py:21
  21.0 34.0 %collective-permute-start = (f32[512,256]{1,0:T(8,128)}, f32[512,256]{1,0:T(8,128)S(1)}, u32[]{:S(2)}, u32[]{:S(2)}) collective-permute-start(f32[512,256]{1,0:T(8,128)} %get-tuple-element.21), channel_id=1, source_target_pairs={{1,0},{2,1},{3,2},{4,3},{5,4},{6,5},{7,6},{9,8},{10,9},{11,10},{12... | collective-permute-start | bytes 1572872 | tf_op jit(solution)/shard_map/ppermute | solution.py:21
  41.7 24.2 %collective-permute-start.5 = (f32[512,256]{1,0:T(8,128)}, f32[512,256]{1,0:T(8,128)S(1)}, u32[]{:S(2)}, u32[]{:S(2)}) collective-permute-start(f32[512,256]{1,0:T(8,128)} %get-tuple-element.28), channel_id=1, source_target_pairs={{0,1},{1,2},{2,3},{3,4},{4,5},{5,6},{6,7},{8,9},{9,10},{10,11},{11... | collective-permute-start | bytes 1572872 | tf_op jit(solution)/shard_map/ppermute | solution.py:21
  59.1 29.9 %collective-permute-start.1 = (f32[512,256]{1,0:T(8,128)}, f32[512,256]{1,0:T(8,128)S(1)}, u32[]{:S(2)}, u32[]{:S(2)}) collective-permute-start(f32[512,256]{1,0:T(8,128)} %get-tuple-element.22), channel_id=1, source_target_pairs={{0,1},{1,2},{2,3},{3,4},{4,5},{5,6},{6,7},{8,9},{9,10},{10,11},{11... | collective-permute-start | bytes 1572872 | tf_op jit(solution)/shard_map/ppermute | solution.py:21
  84.1 23.7 %collective-permute-start.6 = (f32[4,512,128]{2,1,0:T(8,128)}, f32[4,512,128]{2,1,0:T(8,128)}, u32[]{:S(2)}, u32[]{:S(2)}) collective-permute-start(f32[4,512,128]{2,1,0:T(8,128)} %get-tuple-element.31), channel_id=1, source_target_pairs={{0,8},{8,0},{16,24},{24,16},{1,9},{9,1},{17,25},{25,17},{2,10},{10... | collective-permute-start | bytes 3145736 | tf_op jit(solution)/shard_map/ppermute | solution.py:25
  88.4 22.4 %copy-start.2 = (f32[4,512,128]{2,1,0:T(8,128)S(1)}, f32[4,512,128]{2,1,0:T(8,128)}, u32[]{:S(2)}) copy-start(f32[4,512,128]{2,1,0:T(8,128)} %get-tuple-element.36) | copy-start | bytes 3145732
  88.5 22.4 %collective-permute-start.19 = (f32[4,512,128]{2,1,0:T(8,128)}, f32[4,512,128]{2,1,0:T(8,128)S(1)}, u32[]{:S(2)}, u32[]{:S(2)}) collective-permute-start(f32[4,512,128]{2,1,0:T(8,128)} %get-tuple-element.37), channel_id=1, source_target_pairs={{0,8},{8,0},{16,24},{24,16},{1,9},{9,1},{17,25},{25,17},{2,10},{10... | collective-permute-start | bytes 3145736 | tf_op jit(solution)/shard_map/ppermute | solution.py:25
  107.2 4.2 %collective-permute-start.2 = (f32[4,512,128]{2,1,0:T(8,128)}, f32[4,512,128]{2,1,0:T(8,128)}, u32[]{:S(2)}, u32[]{:S(2)}) collective-permute-start(f32[4,512,128]{2,1,0:T(8,128)} %get-tuple-element.25), channel_id=1, source_target_pairs={{0,8},{8,0},{16,24},{24,16},{1,9},{9,1},{17,25},{25,17},{2,10},{10... | collective-permute-start | bytes 3145736 | tf_op jit(solution)/shard_map/ppermute | solution.py:25
  107.3 7.0 %collective-permute-start.17 = (f32[4,512,128]{2,1,0:T(8,128)}, f32[4,512,128]{2,1,0:T(8,128)}, u32[]{:S(2)}, u32[]{:S(2)}) collective-permute-start(f32[4,512,128]{2,1,0:T(8,128)} %get-tuple-element.35), channel_id=1, source_target_pairs={{0,8},{8,0},{16,24},{24,16},{1,9},{9,1},{17,25},{25,17},{2,10},{10... | collective-permute-start | bytes 3145736 | tf_op jit(solution)/shard_map/ppermute | solution.py:25
  107.8 38.7 %copy-start.5 = (f32[4,512,128]{2,1,0:T(8,128)S(1)}, f32[4,512,128]{2,1,0:T(8,128)}, u32[]{:S(2)}) copy-start(f32[4,512,128]{2,1,0:T(8,128)} %get-tuple-element.24) | copy-start | bytes 3145732
  109.2 14.9 %collective-permute-start.7 = (f32[2,512,128]{2,1,0:T(8,128)S(1)}, f32[2,512,128]{2,1,0:T(8,128)S(1)}, u32[]{:S(2)}, u32[]{:S(2)}) collective-permute-start(f32[2,512,128]{2,1,0:T(8,128)S(1)} %slice_add_fusion.4), channel_id=1, source_target_pairs={{0,16},{8,24},{16,0},{24,8},{1,17},{9,25},{17,1},{25,9},{2,18},{10... | collective-permute-start | bytes 1572872 | tf_op jit(solution)/shard_map/ppermute | solution.py:25
  110.9 38.8 %collective-permute-start.20 = (f32[2,512,128]{2,1,0:T(8,128)S(1)}, f32[2,512,128]{2,1,0:T(8,128)S(1)}, u32[]{:S(2)}, u32[]{:S(2)}) collective-permute-start(f32[2,512,128]{2,1,0:T(8,128)S(1)} %slice_add_fusion), channel_id=1, source_target_pairs={{0,16},{8,24},{16,0},{24,8},{1,17},{9,25},{17,1},{25,9},{2,18},{10... | collective-permute-start | bytes 1572872 | tf_op jit(solution)/shard_map/ppermute | solution.py:25
  112.7 33.9 %collective-permute-start.3 = (f32[2,512,128]{2,1,0:T(8,128)S(1)}, f32[2,512,128]{2,1,0:T(8,128)S(1)}, u32[]{:S(2)}, u32[]{:S(2)}) collective-permute-start(f32[2,512,128]{2,1,0:T(8,128)S(1)} %slice_add_fusion.6), channel_id=1, source_target_pairs={{0,16},{8,24},{16,0},{24,8},{1,17},{9,25},{17,1},{25,9},{2,18},{10... | collective-permute-start | bytes 1572872 | tf_op jit(solution)/shard_map/ppermute | solution.py:25
  115.4 41.5 %collective-permute-start.18 = (f32[2,512,128]{2,1,0:T(8,128)S(1)}, f32[2,512,128]{2,1,0:T(8,128)S(1)}, u32[]{:S(2)}, u32[]{:S(2)}) collective-permute-start(f32[2,512,128]{2,1,0:T(8,128)S(1)} %slice_add_fusion.2), channel_id=1, source_target_pairs={{0,16},{8,24},{16,0},{24,8},{1,17},{9,25},{17,1},{25,9},{2,18},{10... | collective-permute-start | bytes 1572872 | tf_op jit(solution)/shard_map/ppermute | solution.py:25
  149.6 10.4 %collective-permute-start.8 = (f32[128,256]{1,0:T(8,128)S(1)}, f32[128,256]{1,0:T(8,128)S(1)}, u32[]{:S(2)}, u32[]{:S(2)}) collective-permute-start(f32[128,256]{1,0:T(8,128)S(1)} %constant_dynamic-slice_fusion.5), channel_id=1, source_target_pairs={{0,8},{8,0},{16,24},{24,16},{1,9},{9,1},{17,25},{25,17},{2,10},{10... | collective-permute-start | bytes 393224 | tf_op jit(solution)/shard_map/ppermute | solution.py:25
  159.9 1.7 collective-permute-start.21
  160.0 4.6 %collective-permute-start.9 = (f32[64,256]{1,0:T(8,128)S(1)}, f32[64,256]{1,0:T(8,128)S(1)}, u32[]{:S(2)}, u32[]{:S(2)}) collective-permute-start(f32[64,256]{1,0:T(8,128)S(1)} %constant_dynamic-slice_fusion.4), channel_id=1, source_target_pairs={{0,16},{8,24},{16,0},{24,8},{1,17},{9,25},{17,1},{25,9},{2,18},{10... | collective-permute-start | bytes 196616 | tf_op jit(solution)/shard_map/ppermute | solution.py:25
  161.7 9.9 %collective-permute-start.22 = (f32[64,256]{1,0:T(8,128)S(1)}, f32[64,256]{1,0:T(8,128)S(1)}, u32[]{:S(2)}, u32[]{:S(2)}) collective-permute-start(f32[64,256]{1,0:T(8,128)S(1)} %constant_dynamic-slice_fusion.1), channel_id=1, source_target_pairs={{0,16},{8,24},{16,0},{24,8},{1,17},{9,25},{17,1},{25,9},{2,18},{10... | collective-permute-start | bytes 196616 | tf_op jit(solution)/shard_map/ppermute | solution.py:25
  164.7 8.8 %collective-permute-start.10 = (f32[32,256]{1,0:T(8,128)S(1)}, f32[32,256]{1,0:T(8,128)S(1)}, u32[]{:S(2)}, u32[]{:S(2)}) collective-permute-start(f32[32,256]{1,0:T(8,128)S(1)} %constant_dynamic-slice_fusion.3), channel_id=1, source_target_pairs={{0,1},{1,0},{2,3},{3,2},{4,5},{5,4},{6,7},{7,6},{8,9},{9,8},{10,11... | collective-permute-start | bytes 98312 | tf_op jit(solution)/shard_map/ppermute | solution.py:25
  171.6 6.3 %collective-permute-start.23 = (f32[32,256]{1,0:T(8,128)S(1)}, f32[32,256]{1,0:T(8,128)S(1)}, u32[]{:S(2)}, u32[]{:S(2)}) collective-permute-start(f32[32,256]{1,0:T(8,128)S(1)} %constant_dynamic-slice_fusion), channel_id=1, source_target_pairs={{0,1},{1,0},{2,3},{3,2},{4,5},{5,4},{6,7},{7,6},{8,9},{9,8},{10,11... | collective-permute-start | bytes 98312 | tf_op jit(solution)/shard_map/ppermute | solution.py:25
  173.5 7.1 %collective-permute-start.13 = (f32[32,256]{1,0:T(8,128)S(1)}, f32[32,256]{1,0:T(8,128)S(1)}, u32[]{:S(2)}, u32[]{:S(2)}) collective-permute-start(f32[32,256]{1,0:T(8,128)S(1)} %dynamic-slice_add_fusion.5), channel_id=1, source_target_pairs={{0,6},{1,7},{2,4},{3,5},{4,2},{5,3},{6,0},{7,1},{8,14},{9,15},{10,... | collective-permute-start | bytes 98312 | tf_op jit(solution)/shard_map/ppermute | solution.py:25
  176.1 6.3 %collective-permute-start.12 = (f32[32,256]{1,0:T(8,128)S(1)}, f32[32,256]{1,0:T(8,128)S(1)}, u32[]{:S(2)}, u32[]{:S(2)}) collective-permute-start(f32[32,256]{1,0:T(8,128)S(1)} %dynamic-slice_add_fusion.5), channel_id=1, source_target_pairs={{0,4},{1,5},{2,6},{3,7},{4,0},{5,1},{6,2},{7,3},{8,12},{9,13},{10,... | collective-permute-start | bytes 98312 | tf_op jit(solution)/shard_map/ppermute | solution.py:25
  176.5 5.8 %collective-permute-start.11 = (f32[32,256]{1,0:T(8,128)S(1)}, f32[32,256]{1,0:T(8,128)S(1)}, u32[]{:S(2)}, u32[]{:S(2)}) collective-permute-start(f32[32,256]{1,0:T(8,128)S(1)} %dynamic-slice_add_fusion.5), channel_id=1, source_target_pairs={{0,2},{1,3},{2,0},{3,1},{4,6},{5,7},{6,4},{7,5},{8,10},{9,11},{10,... | collective-permute-start | bytes 98312 | tf_op jit(solution)/shard_map/ppermute | solution.py:25
  177.9 6.6 %collective-permute-start.26 = (f32[32,256]{1,0:T(8,128)S(1)}, f32[32,256]{1,0:T(8,128)S(1)}, u32[]{:S(2)}, u32[]{:S(2)}) collective-permute-start(f32[32,256]{1,0:T(8,128)S(1)} %dynamic-slice_add_fusion.4), channel_id=1, source_target_pairs={{0,6},{1,7},{2,4},{3,5},{4,2},{5,3},{6,0},{7,1},{8,14},{9,15},{10,... | collective-permute-start | bytes 98312 | tf_op jit(solution)/shard_map/ppermute | solution.py:25
  180.5 4.8 %collective-permute-start.25 = (f32[32,256]{1,0:T(8,128)S(1)}, f32[32,256]{1,0:T(8,128)S(1)}, u32[]{:S(2)}, u32[]{:S(2)}) collective-permute-start(f32[32,256]{1,0:T(8,128)S(1)} %dynamic-slice_add_fusion.4), channel_id=1, source_target_pairs={{0,4},{1,5},{2,6},{3,7},{4,0},{5,1},{6,2},{7,3},{8,12},{9,13},{10,... | collective-permute-start | bytes 98312 | tf_op jit(solution)/shard_map/ppermute | solution.py:25
  180.5 4.8 %collective-permute-start.24 = (f32[32,256]{1,0:T(8,128)S(1)}, f32[32,256]{1,0:T(8,128)S(1)}, u32[]{:S(2)}, u32[]{:S(2)}) collective-permute-start(f32[32,256]{1,0:T(8,128)S(1)} %dynamic-slice_add_fusion.4), channel_id=1, source_target_pairs={{0,2},{1,3},{2,0},{3,1},{4,6},{5,7},{6,4},{7,5},{8,10},{9,11},{10,... | collective-permute-start | bytes 98312 | tf_op jit(solution)/shard_map/ppermute | solution.py:25
  182.3 4.1 %collective-permute-start.14 = (f32[32,256]{1,0:T(8,128)S(1)}, f32[32,256]{1,0:T(8,128)S(1)}, u32[]{:S(2)}, u32[]{:S(2)}) collective-permute-start(f32[32,256]{1,0:T(8,128)S(1)} %add_add_fusion.1), channel_id=1, source_target_pairs={{0,1},{1,0},{2,3},{3,2},{4,5},{5,4},{6,7},{7,6},{8,9},{9,8},{10,11... | collective-permute-start | bytes 98312 | tf_op jit(solution)/shard_map/ppermute | solution.py:25
  185.4 4.0 %collective-permute-start.27 = (f32[32,256]{1,0:T(8,128)S(1)}, f32[32,256]{1,0:T(8,128)S(1)}, u32[]{:S(2)}, u32[]{:S(2)}) collective-permute-start(f32[32,256]{1,0:T(8,128)S(1)} %add_add_fusion), channel_id=1, source_target_pairs={{0,1},{1,0},{2,3},{3,2},{4,5},{5,4},{6,7},{7,6},{8,9},{9,8},{10,11... | collective-permute-start | bytes 98312 | tf_op jit(solution)/shard_map/ppermute | solution.py:25
  186.4 4.9 %collective-permute-start.15 = (f32[64,256]{1,0:T(8,128)S(1)}, f32[64,256]{1,0:T(8,128)S(1)}, u32[]{:S(2)}, u32[]{:S(2)}) collective-permute-start(f32[64,256]{1,0:T(8,128)S(1)} %maximum_select_fusion.4), channel_id=1, source_target_pairs={{0,16},{8,24},{16,0},{24,8},{1,17},{9,25},{17,1},{25,9},{2,18},{10... | collective-permute-start | bytes 196616 | tf_op jit(solution)/shard_map/ppermute | solution.py:25
  189.3 4.3 %collective-permute-start.28 = (f32[64,256]{1,0:T(8,128)S(1)}, f32[64,256]{1,0:T(8,128)S(1)}, u32[]{:S(2)}, u32[]{:S(2)}) collective-permute-start(f32[64,256]{1,0:T(8,128)S(1)} %maximum_select_fusion.5), channel_id=1, source_target_pairs={{0,16},{8,24},{16,0},{24,8},{1,17},{9,25},{17,1},{25,9},{2,18},{10... | collective-permute-start | bytes 196616 | tf_op jit(solution)/shard_map/ppermute | solution.py:25
  191.4 2.4 %collective-permute-start.16 = (f32[128,256]{1,0:T(8,128)S(1)}, f32[128,256]{1,0:T(8,128)S(1)}, u32[]{:S(2)}, u32[]{:S(2)}) collective-permute-start(f32[128,256]{1,0:T(8,128)S(1)} %maximum_select_fusion.2), channel_id=1, source_target_pairs={{0,8},{8,0},{16,24},{24,16},{1,9},{9,1},{17,25},{25,17},{2,10},{10... | collective-permute-start | bytes 393224 | tf_op jit(solution)/shard_map/ppermute | solution.py:25
  193.7 14.7 %collective-permute-start.29 = (f32[128,256]{1,0:T(8,128)S(1)}, f32[128,256]{1,0:T(8,128)S(1)}, u32[]{:S(2)}, u32[]{:S(2)}) collective-permute-start(f32[128,256]{1,0:T(8,128)S(1)} %maximum_select_fusion.3), channel_id=1, source_target_pairs={{0,8},{8,0},{16,24},{24,16},{1,9},{9,1},{17,25},{25,17},{2,10},{10... | collective-permute-start | bytes 393224 | tf_op jit(solution)/shard_map/ppermute | solution.py:25
  (7 other events, 34.8 us)

commit v3 on v2

--- a/solution.py
+++ b/solution.py
@@ -186,43 +186,49 @@
     )(s_times, top_next, factors, coupled)
 
 
-def above_kernel(last_ref, below_ref, next_ref, i_hbm, u_hbm, added_ref, wv, uv, sem):
+def above_kernel(parts, below_hbm, next_hbm, i_hbm, u_hbm, added_ref, below, top_next, wv, uv, sem):
     copies = (
-        pltpu.make_async_copy(i_hbm.at[2], wv, sem.at[0]),
-        pltpu.make_async_copy(u_hbm.at[u_hbm.shape[0] - 1], uv, sem.at[1]),
+        pltpu.make_async_copy(below_hbm, below, sem.at[0]),
+        pltpu.make_async_copy(i_hbm.at[2], wv, sem.at[1]),
+        pltpu.make_async_copy(next_hbm, top_next, sem.at[2]),
+        pltpu.make_async_copy(u_hbm.at[u_hbm.shape[0] - 1], uv, sem.at[3]),
     )
     for copy in copies:
         copy.start()
-    copies[0].wait()
-    above = next_ref[...] - complex_apply(wv[...], below_ref[...])
-    above = jnp.where(last_ref[0] == 1, jnp.zeros_like(above), above)
-    copies[1].wait()
+    for copy in copies[:3]:
+        copy.wait()
+    above = top_next[...] - complex_apply(wv[...], below[...])
+    topmost = lax.axis_index("dom") == parts - 1
+    above = jnp.where(topmost, jnp.zeros_like(above), above)
+    copies[3].wait()
     added_ref[...] = real_apply(uv[...], above)
 
 
-def interface_above(topmost, below, top_next, factors, coupled):
+def interface_above(parts, below, top_next, factors, coupled):
     order, width = top_next.shape
     vmem = pl.BlockSpec(memory_space=pltpu.VMEM)
     hbm = pl.BlockSpec(memory_space=pl.ANY)
     return pl.pallas_call(
-        above_kernel,
+        functools.partial(above_kernel, parts),
         out_shape=jax.ShapeDtypeStruct(top_next.shape, F32),
-        in_specs=[pl.BlockSpec(memory_space=pltpu.SMEM), vmem, vmem, hbm, hbm],
+        in_specs=[hbm] * 4,
         out_specs=vmem,
         scratch_shapes=[
+            pltpu.VMEM(top_next.shape, F32),
+            pltpu.VMEM(top_next.shape, F32),
             pltpu.VMEM((2 * order, order), BF16),
             pltpu.VMEM((order, order), BF16),
-            pltpu.SemaphoreType.DMA((2,)),
+            pltpu.SemaphoreType.DMA((4,)),
         ],
         cost_estimate=pl.CostEstimate(
             flops=6 * order * order * width, transcendentals=0, bytes_accessed=4 * 2**20
         ),
         name="interface_above",
-    )(topmost, below, top_next, factors, coupled)
+    )(below, top_next, factors, coupled)
 
 
 def second_kernel(
-    lane, owners, place_ref, scale_ref, f_hbm, g_hbm, u_hbm, arrive_hbm, added_hbm,
+    lane, owners, pole_ref, f_hbm, g_hbm, u_hbm, arrive_hbm, added_hbm,
     keep_y, keep_z, send_y, send_z, fv, gv, uv, ut, hold, yv, zv, arrive, added, sem, out_sem, tip_sem,
 ):
     blocks = gv.shape[0]
@@ -271,9 +277,12 @@
     coupled = real_apply(ut[(last + 1) % 2], hold[last - 1])
     hold[last] = complex_apply(gv[last], (given(last) + added[...]) + coupled)
 
-    wr, wi, zwr, zwi = scale_ref[0], scale_ref[1], scale_ref[2], scale_ref[3]
-    low = place_ref[0]
-    high = place_ref[1]
+    zr, zi, wr, wi = (pole_ref[0, i] for i in range(4))
+    zwr = wr * zr - wi * zi
+    zwi = wr * zi + wi * zr
+    pole = lax.axis_index("pole")
+    low = pole % 2
+    high = pole // 2
 
     def emit(k, x):
         real, imag = x[:, :width], x[:, width:]
@@ -310,7 +319,7 @@
         pltpu.make_async_copy(zv.at[k], keep_z.at[0], out_sem.at[1, k]).wait()
 
 
-def second_solve(chunk, width, owners, place, scales, source, inverse, coupled, arriving, added):
+def second_solve(chunk, width, owners, pole_values, source, inverse, coupled, arriving, added):
     blocks, stacked, order = inverse.shape
     part = jax.ShapeDtypeStruct((blocks // 2, order, width), F32)
     hbm = pl.BlockSpec(memory_space=pl.ANY)
@@ -320,7 +329,7 @@
     return pl.pallas_call(
         functools.partial(second_kernel, chunk * width, owners),
         out_shape=(part,) * 4,
-        in_specs=[smem, smem] + [hbm] * 5,
+        in_specs=[smem] + [hbm] * 5,
         out_specs=(hbm,) * 4,
         scratch_shapes=[
             pltpu.VMEM((blocks, order, width), BF16),
@@ -338,7 +347,7 @@
         ],
         cost_estimate=pl.CostEstimate(flops=flops, transcendentals=0, bytes_accessed=16 * 2**20),
         name="second_solve",
-    )(place, scales, source, inverse, coupled, arriving, added)
+    )(pole_values, source, inverse, coupled, arriving, added)
 
 
 def factor_kernel(total, gram_ref, y_ref, basis_ref, inverse_ref, acc):
@@ -422,20 +431,20 @@
     )
 
 
-def summed_everywhere(x, steps, far):
+def summed_everywhere(x, near, far):
     kept = []
-    for axis, mask in steps:
+    for axis, i in near:
         half = x.shape[0] // 2
-        bit = (lax.axis_index(axis) // mask) % 2
-        mine = lax.dynamic_slice_in_dim(x, bit * half, half, 0)
-        other = lax.dynamic_slice_in_dim(x, (1 - bit) * half, half, 0)
-        x = mine + flipped(other, axis, mask)
-        kept.append(bit)
-    axis, masks = far
-    x = x + sum(flipped(x, axis, mask) for mask in masks)
-    for (axis, mask), bit in zip(reversed(steps), reversed(kept)):
-        other = flipped(x, axis, mask)
-        x = jnp.where(bit == 0, jnp.concatenate([x, other]), jnp.concatenate([other, x]))
+        upper = (lax.axis_index(axis) >> i) & 1 == 1
+        mine = jnp.where(upper, x[half:], x[:half])
+        other = jnp.where(upper, x[:half], x[half:])
+        x = mine + flipped(other, axis, 1 << i)
+        kept.append(upper)
+    for axis, i in far:
+        x = x + flipped(x, axis, 1 << i)
+    for (axis, i), upper in zip(reversed(near), reversed(kept)):
+        other = flipped(x, axis, 1 << i)
+        x = jnp.where(upper, jnp.concatenate([other, x]), jnp.concatenate([x, other]))
     return x
 
 
@@ -451,14 +460,6 @@
     coupled = coupling[0]
     inverse = pivots[0, 0].reshape(blocks, 2 * order, order)
     factors = interface[0, 0].reshape(3, 2 * order, order)
-    pole = lax.axis_index("pole")
-    dom = lax.axis_index("dom")
-    topmost = (dom == parts - 1).astype(jnp.int32).reshape(1)
-    place = jnp.stack([pole % 2, pole // 2]).astype(jnp.int32)
-    real_z, imag_z, real_w, imag_w = (pole_values[0, i] for i in range(4))
-    scales = jnp.stack(
-        [real_w, imag_w, real_w * real_z - imag_w * imag_z, real_w * imag_z + imag_w * real_z]
-    )
     chunks = vectors // width
     tips, s_times = first_solve(chunks, source, inverse, coupled, factors)
     tops, belows, arrivals, added = [], [], [], []
@@ -467,7 +468,7 @@
     for c in range(chunks):
         belows.append(interface_below(s_times[c], tops[c], factors, coupled))
         arrivals.append(shifted(belows[c][1], "dom", 1))
-        added.append(interface_above(topmost, belows[c][0], tops[c], factors, coupled))
+        added.append(interface_above(parts, belows[c][0], tops[c], factors, coupled))
     masks = [1 << i for i in range(1, owners.bit_length() - 1)]
 
     def pole_sum(keep, send):
@@ -482,14 +483,15 @@
     own_y, own_z = [], []
     for c in range(chunks):
         keep_y, keep_z, send_y, send_z = second_solve(
-            c, width, owners, place, scales, source, inverse, coupled, arrivals[c], added[c]
+            c, width, owners, pole_values, source, inverse, coupled, arrivals[c], added[c]
         )
         own_y.append(pole_sum(keep_y, send_y))
         own_z.append(pole_sum(keep_z, send_z))
     own_y = jnp.concatenate(own_y, axis=1)
     own_z = jnp.concatenate(own_z, axis=1)
-    near = [("pole", 1 << i) for i in range(owners.bit_length() - 1)] + [("dom", 1)]
-    far = ("dom", tuple(range(2, parts, 2)))
+    near = [("pole", i) for i in range(owners.bit_length() - 1)]
+    near.insert(1, ("dom", 0))
+    far = [("dom", i) for i in range(1, parts.bit_length() - 1)]
     gram = summed_everywhere(inner_products(own_y, own_y), near, far)
     projected = summed_everywhere(inner_products(own_y, own_z), near, far)
     row_total = blocks * order * parts

time: 213 us -> 211 us (level)
  starting transfers between devices: 42.9 us -> 49 us
  between operations: 6.08 us -> 0.97 us
  other arithmetic: 12.5 us -> 9.96 us
  waiting for transfers between devices: 57.1 us -> 59.6 us
    ppermute x26 -> x24, starting transfers between devices: 32.9 us -> 36.9 us  [flipped(): lax.ppermute(x, axis, [(i, i ^ mask) for i in range(lax.axis_size(axis))])]
    another operation x2 -> x0, other arithmetic: 2.65 us -> none  [the longest x1 1.99 us: on_device(): jnp.stack([real_w, imag_w, real_w * real_z - imag_w * imag_z, real_w * im...]
    ppermute x26 -> x24, waiting for transfers between devices: 41.8 us -> 43 us  [flipped(): lax.ppermute(x, axis, [(i, i ^ mask) for i in range(lax.axis_size(axis))])]
  transfers between devices with their start and end apart: 30 -> 28, of which waited for: 9 -> 12; matrix products, arithmetic and copies ran while one was open for 8% -> 6% of each run, Pallas kernels for 30% -> 29%
where the time goes in v3:
time: 211 us; the launch traced here: 210 us
  Pallas kernels  83.7 us (40%)
  waiting for transfers between devices  59.6 us (28%)
  starting transfers between devices  49 us (23%)
  other arithmetic  9.96 us (5%)
  matrix products  3.66 us (2%)
  local copies, waits for them, and re-layouts  3.25 us (2%)
    ppermute x24, waiting for transfers between devices, flipped(): lax.ppermute(x, axis, [(i, i ^ mask) for i in range(lax.axis_size(axis))])  43 us
    ppermute x24, starting transfers between devices, flipped(): lax.ppermute(x, axis, [(i, i ^ mask) for i in range(lax.axis_size(axis))])  36.9 us
    pallas_call x2, Pallas kernels, second_solve(): pl.pallas_call(functools.partial(second_kernel, chunk * width, owners), o...  34.8 us
    pallas_call x1, Pallas kernels, first_solve(): pl.pallas_call(functools.partial(first_kernel, groups), out_shape=(tip,)...  19.1 us
    ppermute x4, waiting for transfers between devices, shifted(): return lax.ppermute(x, axis, pairs)  16.6 us
    pallas_call x1, Pallas kernels, orthonormalized(): pl.pallas_call(functools.partial(factor_kernel, float(total)), out_shape=...  13.9 us
    ppermute x4, starting transfers between devices, shifted(): return lax.ppermute(x, axis, pairs)  12.1 us
    pallas_call x2, Pallas kernels, interface_above(): pl.pallas_call(functools.partial(above_kernel, parts), out_shape=jax.Shap...  6.68 us
  transfers between devices with their start and end apart: 28, of which 12 were waited for; matrix products, arithmetic and copies ran while one was open for 6% of the time, Pallas kernels for 29%

profile of v3, /device:TPU:0, one launch (start us, length us, event | category | flops | bytes accessed | tf_op | source)
XLA Modules:
  0.0 210.2 jit_solution(1081140788566607234)
XLA Ops:
  0.6 19.1 %first_solve.1 = (f32[512,256]{1,0:T(8,128)}, f32[512,256]{1,0:T(8,128)}, f32[512,256]{1,0:T(8,128)}, f32[512,256]{1,0:T(8,128)}) custom-call(bf16[8,512,256]{2,1,0:T(8,128)(2,1)} %bitcast.32, bf16[8,1024,512]{2,1,0:T(8,128)(2,1)} %bitcast.29, bf16[8,512,512]{2,1,0:T(8,128)(2,1)} %bitcast.9, bf16[3,1024,512]{2,1,0:T(8,128)(2,1)} %bitcast.16), custom_call_target="tpu_custom_call" | custom-call | flops 9932111872 | bytes 14680064 | tf_op jit(solution)/shard_map/first_solve/pallas_call | solution.py:125
  22.3 15.3 %collective-permute-done.4.next_hbm = f32[512,256]{1,0:T(8,128)S(1)} collective-permute-done((f32[512,256]{1,0:T(8,128)}, f32[512,256]{1,0:T(8,128)S(1)}, u32[]{:S(2)}, u32[]{:S(2)}) %collective-permute-start.4) | collective-permute-done | bytes 524320 | tf_op jit(solution)/shard_map/ppermute | solution.py:21
  38.4 3.3 %interface_below.3 = (f32[512,256]{1,0:T(8,128)}, f32[512,256]{1,0:T(8,128)}) custom-call(f32[512,256]{1,0:T(8,128)} %get-tuple-element.26.sb_hbm, f32[512,256]{1,0:T(8,128)} %copy-done.1, bf16[3,1024,512]{2,1,0:T(8,128)(2,1)} %bitcast.17, bf16[8,512,512]{2,1,0:T(8,128)(2,1)} %bitcast.10), custom_call_target="tpu_custom_call" | custom-call | flops 402653184 | bytes 4194304 | tf_op jit(solution)/shard_map/interface_below/pallas_call | solution.py:170
  41.7 4.8 %collective-permute-start.5 = (f32[512,256]{1,0:T(8,128)}, f32[512,256]{1,0:T(8,128)S(1)}, u32[]{:S(2)}, u32[]{:S(2)}) collective-permute-start(f32[512,256]{1,0:T(8,128)} %get-tuple-element.28), channel_id=1, source_target_pairs={{0,1},{1,2},{2,3},{3,4},{4,5},{5,6},{6,7},{8,9},{9,10},{10,11},{11... | collective-permute-start | bytes 1572872 | tf_op jit(solution)/shard_map/ppermute | solution.py:21
  48.7 3.3 %interface_below.2 = (f32[512,256]{1,0:T(8,128)}, f32[512,256]{1,0:T(8,128)}) custom-call(f32[512,256]{1,0:T(8,128)} %get-tuple-element.20.sb_hbm, f32[512,256]{1,0:T(8,128)} %copy-done, bf16[3,1024,512]{2,1,0:T(8,128)(2,1)} %bitcast.18, bf16[8,512,512]{2,1,0:T(8,128)(2,1)} %bitcast.11), custom_call_target="tpu_custom_call" | custom-call | flops 402653184 | bytes 4194304 | tf_op jit(solution)/shard_map/interface_below/pallas_call | solution.py:170
  52.0 4.7 %collective-permute-start.1 = (f32[512,256]{1,0:T(8,128)}, f32[512,256]{1,0:T(8,128)S(1)}, u32[]{:S(2)}, u32[]{:S(2)}) collective-permute-start(f32[512,256]{1,0:T(8,128)} %get-tuple-element.22), channel_id=1, source_target_pairs={{0,1},{1,2},{2,3},{3,4},{4,5},{5,6},{6,7},{8,9},{9,10},{10,11},{11... | collective-permute-start | bytes 1572872 | tf_op jit(solution)/shard_map/ppermute | solution.py:21
  56.7 3.3 %interface_above.3.added_hbm = f32[512,256]{1,0:T(8,128)} custom-call(f32[512,256]{1,0:T(8,128)} %get-tuple-element.29.below_hbm, f32[512,256]{1,0:T(8,128)} %copy-done.1, bf16[3,1024,512]{2,1,0:T(8,128)(2,1)} %bitcast.19, bf16[8,512,512]{2,1,0:T(8,128)(2,1)} %bitcast.12), custom_call_target="tpu_custom_call" | custom-call | flops 402653184 | bytes 4194304 | tf_op jit(solution)/shard_map/interface_above/pallas_call | solution.py:211
  60.8 17.4 %second_solve.3 = (f32[4,512,128]{2,1,0:T(8,128)}, f32[4,512,128]{2,1,0:T(8,128)}, f32[4,512,128]{2,1,0:T(8,128)}, f32[4,512,128]{2,1,0:T(8,128)}) custom-call(f32[1,4]{1,0:T(1,128)} %pole_ref.3, bf16[8,512,256]{2,1,0:T(8,128)(2,1)} %bitcast.33, bf16[8,1024,512]{2,1,0:T(8,128)(2,1)} %bitcast.30, bf16[8,512,512]{2,1,0:T(8,128)(2,1)} %bitcast.13, ...), custom_call_target="tpu_custom_call" | custom-call | flops 4966055936 | bytes 16777216 | tf_op jit(solution)/shard_map/second_solve/pallas_call | solution.py:329
  78.3 3.4 %interface_above.2.added_hbm = f32[512,256]{1,0:T(8,128)} custom-call(f32[512,256]{1,0:T(8,128)} %get-tuple-element.23.below_hbm, f32[512,256]{1,0:T(8,128)} %copy-done, bf16[3,1024,512]{2,1,0:T(8,128)(2,1)} %bitcast.20, bf16[8,512,512]{2,1,0:T(8,128)(2,1)} %bitcast.14), custom_call_target="tpu_custom_call" | custom-call | flops 402653184 | bytes 4194304 | tf_op jit(solution)/shard_map/interface_above/pallas_call | solution.py:211
  83.0 17.4 %second_solve.2 = (f32[4,512,128]{2,1,0:T(8,128)}, f32[4,512,128]{2,1,0:T(8,128)}, f32[4,512,128]{2,1,0:T(8,128)}, f32[4,512,128]{2,1,0:T(8,128)}) custom-call(f32[1,4]{1,0:T(1,128)} %pole_ref.3, bf16[8,512,256]{2,1,0:T(8,128)(2,1)} %bitcast.34, bf16[8,1024,512]{2,1,0:T(8,128)(2,1)} %bitcast.31, bf16[8,512,512]{2,1,0:T(8,128)(2,1)} %bitcast.15, ...), custom_call_target="tpu_custom_call" | custom-call | flops 4966055936 | bytes 16777216 | tf_op jit(solution)/shard_map/second_solve/pallas_call | solution.py:329
  102.4 1.6 collective-permute-start.7
  105.9 1.6 collective-permute-start.3
  109.2 8.1 %collective-permute-done.7 = f32[2,512,128]{2,1,0:T(8,128)S(1)} collective-permute-done((f32[2,512,128]{2,1,0:T(8,128)S(1)}, f32[2,512,128]{2,1,0:T(8,128)S(1)}, u32[]{:S(2)}, u32[]{:S(2)}) %collective-permute-start.7) | collective-permute-done | bytes 524320 | tf_op jit(solution)/shard_map/ppermute | solution.py:25
  118.4 21.4 %collective-permute-done.3 = f32[2,512,128]{2,1,0:T(8,128)S(1)} collective-permute-done((f32[2,512,128]{2,1,0:T(8,128)S(1)}, f32[2,512,128]{2,1,0:T(8,128)S(1)}, u32[]{:S(2)}, u32[]{:S(2)}) %collective-permute-start.3) | collective-permute-done | bytes 524320 | tf_op jit(solution)/shard_map/ppermute | solution.py:25
  140.9 1.8 fusion.9
  142.9 7.2 %collective-permute-done.17 = f32[2,512,128]{2,1,0:T(8,128)S(1)} collective-permute-done((f32[2,512,128]{2,1,0:T(8,128)S(1)}, f32[2,512,128]{2,1,0:T(8,128)S(1)}, u32[]{:S(2)}, u32[]{:S(2)}) %collective-permute-start.17) | collective-permute-done | bytes 524320 | tf_op jit(solution)/shard_map/ppermute | solution.py:25
  151.2 1.8 fusion
  153.2 11.8 %collective-permute-start.9 = (f32[64,256]{1,0:T(8,128)S(1)}, f32[64,256]{1,0:T(8,128)S(1)}, u32[]{:S(2)}, u32[]{:S(2)}) collective-permute-start(f32[64,256]{1,0:T(8,128)S(1)} %slice_select_fusion.3), channel_id=1, source_target_pairs={{0,1},{1,0},{2,3},{3,2},{4,5},{5,4},{6,7},{7,6},{8,9},{9,8},{10,11... | collective-permute-start | bytes 196616 | tf_op jit(solution)/shard_map/ppermute | solution.py:25
  166.4 1.4 collective-permute-done.9
  167.8 1.6 collective-permute-start.10
  169.5 1.6 collective-permute-start.22
  171.9 1.6 collective-permute-start.11
  173.5 1.6 collective-permute-start.23
  175.8 2.6 %collective-permute-start.12 = (f32[32,256]{1,0:T(8,128)S(1)}, f32[32,256]{1,0:T(8,128)S(1)}, u32[]{:S(2)}, u32[]{:S(2)}) collective-permute-start(f32[32,256]{1,0:T(8,128)S(1)} %add.75), channel_id=1, source_target_pairs={{0,4},{1,5},{2,6},{3,7},{4,0},{5,1},{6,2},{7,3},{8,12},{9,13},{10,... | collective-permute-start | bytes 98312 | tf_op jit(solution)/shard_map/ppermute | solution.py:25
  178.4 1.7 collective-permute-start.24
  180.6 1.5 collective-permute-start.13
  182.2 1.5 collective-permute-done.24
  183.7 1.5 collective-permute-start.25
  185.2 2.2 %collective-permute-start.14 = (f32[64,256]{1,0:T(8,128)S(1)}, f32[64,256]{1,0:T(8,128)S(1)}, u32[]{:S(2)}, u32[]{:S(2)}) collective-permute-start(f32[64,256]{1,0:T(8,128)S(1)} %maximum_select_fusion.4), channel_id=1, source_target_pairs={{0,1},{1,0},{2,3},{3,2},{4,5},{5,4},{6,7},{7,6},{8,9},{9,8},{10,11... | collective-permute-start | bytes 196616 | tf_op jit(solution)/shard_map/ppermute | solution.py:25
  187.6 2.1 %collective-permute-start.26 = (f32[64,256]{1,0:T(8,128)S(1)}, f32[64,256]{1,0:T(8,128)S(1)}, u32[]{:S(2)}, u32[]{:S(2)}) collective-permute-start(f32[64,256]{1,0:T(8,128)S(1)} %maximum_select_fusion.5), channel_id=1, source_target_pairs={{0,1},{1,0},{2,3},{3,2},{4,5},{5,4},{6,7},{7,6},{8,9},{9,8},{10,11... | collective-permute-start | bytes 196616 | tf_op jit(solution)/shard_map/ppermute | solution.py:25
  192.8 13.9 %orthonormalized.1 = (f32[1024,256]{1,0:T(8,128)}, f32[256,256]{1,0:T(8,128)}) custom-call(f32[256,256]{1,0:T(8,128)} %maximum_select_fusion.gram_ref, f32[1024,256]{1,0:T(8,128)} %pad_maximum_fusion.y_ref), custom_call_target="tpu_custom_call" | custom-call | flops 12884901888 | bytes 3145728 | tf_op jit(solution)/shard_map/orthonormalized/pallas_call | solution.py:411
  207.5 2.7 %congruence.1 = f32[256,256]{1,0:T(8,128)} custom-call(f32[256,256]{1,0:T(8,128)} %get-tuple-element.33.inverse_ref, f32[256,256]{1,0:T(8,128)} %maximum_select_fusion.1.proj_ref), custom_call_target="tpu_custom_call" | custom-call | flops 1073741824 | bytes 1048576 | tf_op jit(solution)/shard_map/congruence/pallas_call | solution.py:398
  (82 shorter events, 24.5 us)
Async XLA Ops:
  19.7 17.9 %collective-permute-start.4 = (f32[512,256]{1,0:T(8,128)}, f32[512,256]{1,0:T(8,128)S(1)}, u32[]{:S(2)}, u32[]{:S(2)}) collective-permute-start(f32[512,256]{1,0:T(8,128)} %get-tuple-element.27), channel_id=1, source_target_pairs={{1,0},{2,1},{3,2},{4,3},{5,4},{6,5},{7,6},{9,8},{10,9},{11,10},{12... | collective-permute-start | bytes 1572872 | tf_op jit(solution)/shard_map/ppermute | solution.py:21
  21.0 26.9 %collective-permute-start = (f32[512,256]{1,0:T(8,128)}, f32[512,256]{1,0:T(8,128)S(1)}, u32[]{:S(2)}, u32[]{:S(2)}) collective-permute-start(f32[512,256]{1,0:T(8,128)} %get-tuple-element.21), channel_id=1, source_target_pairs={{1,0},{2,1},{3,2},{4,3},{5,4},{6,5},{7,6},{9,8},{10,9},{11,10},{12... | collective-permute-start | bytes 1572872 | tf_op jit(solution)/shard_map/ppermute | solution.py:21
  41.7 18.3 %collective-permute-start.5 = (f32[512,256]{1,0:T(8,128)}, f32[512,256]{1,0:T(8,128)S(1)}, u32[]{:S(2)}, u32[]{:S(2)}) collective-permute-start(f32[512,256]{1,0:T(8,128)} %get-tuple-element.28), channel_id=1, source_target_pairs={{0,1},{1,2},{2,3},{3,4},{4,5},{5,6},{6,7},{8,9},{9,10},{10,11},{11... | collective-permute-start | bytes 1572872 | tf_op jit(solution)/shard_map/ppermute | solution.py:21
  52.0 30.2 %collective-permute-start.1 = (f32[512,256]{1,0:T(8,128)}, f32[512,256]{1,0:T(8,128)S(1)}, u32[]{:S(2)}, u32[]{:S(2)}) collective-permute-start(f32[512,256]{1,0:T(8,128)} %get-tuple-element.22), channel_id=1, source_target_pairs={{0,1},{1,2},{2,3},{3,4},{4,5},{5,6},{6,7},{8,9},{9,10},{10,11},{11... | collective-permute-start | bytes 1572872 | tf_op jit(solution)/shard_map/ppermute | solution.py:21
  78.2 22.8 %collective-permute-start.6 = (f32[4,512,128]{2,1,0:T(8,128)}, f32[4,512,128]{2,1,0:T(8,128)}, u32[]{:S(2)}, u32[]{:S(2)}) collective-permute-start(f32[4,512,128]{2,1,0:T(8,128)} %get-tuple-element.31), channel_id=1, source_target_pairs={{0,8},{8,0},{16,24},{24,16},{1,9},{9,1},{17,25},{25,17},{2,10},{10... | collective-permute-start | bytes 3145736 | tf_op jit(solution)/shard_map/ppermute | solution.py:25
  81.7 22.4 %copy-start.2 = (f32[4,512,128]{2,1,0:T(8,128)S(1)}, f32[4,512,128]{2,1,0:T(8,128)}, u32[]{:S(2)}) copy-start(f32[4,512,128]{2,1,0:T(8,128)} %get-tuple-element.36) | copy-start | bytes 3145732
  81.7 22.4 %collective-permute-start.18 = (f32[4,512,128]{2,1,0:T(8,128)}, f32[4,512,128]{2,1,0:T(8,128)S(1)}, u32[]{:S(2)}, u32[]{:S(2)}) collective-permute-start(f32[4,512,128]{2,1,0:T(8,128)} %get-tuple-element.37), channel_id=1, source_target_pairs={{0,8},{8,0},{16,24},{24,16},{1,9},{9,1},{17,25},{25,17},{2,10},{10... | collective-permute-start | bytes 3145736 | tf_op jit(solution)/shard_map/ppermute | solution.py:25
  100.4 7.1 %copy-start.3 = (f32[4,512,128]{2,1,0:T(8,128)S(1)}, f32[4,512,128]{2,1,0:T(8,128)}, u32[]{:S(2)}) copy-start(f32[4,512,128]{2,1,0:T(8,128)} %get-tuple-element.34) | copy-start | bytes 3145732
  100.5 4.2 %collective-permute-start.2 = (f32[4,512,128]{2,1,0:T(8,128)}, f32[4,512,128]{2,1,0:T(8,128)}, u32[]{:S(2)}, u32[]{:S(2)}) collective-permute-start(f32[4,512,128]{2,1,0:T(8,128)} %get-tuple-element.25), channel_id=1, source_target_pairs={{0,8},{8,0},{16,24},{24,16},{1,9},{9,1},{17,25},{25,17},{2,10},{10... | collective-permute-start | bytes 3145736 | tf_op jit(solution)/shard_map/ppermute | solution.py:25
  100.6 7.0 %collective-permute-start.16 = (f32[4,512,128]{2,1,0:T(8,128)}, f32[4,512,128]{2,1,0:T(8,128)}, u32[]{:S(2)}, u32[]{:S(2)}) collective-permute-start(f32[4,512,128]{2,1,0:T(8,128)} %get-tuple-element.35), channel_id=1, source_target_pairs={{0,8},{8,0},{16,24},{24,16},{1,9},{9,1},{17,25},{25,17},{2,10},{10... | collective-permute-start | bytes 3145736 | tf_op jit(solution)/shard_map/ppermute | solution.py:25
  101.0 16.3 %copy-start.4 = (f32[4,512,128]{2,1,0:T(8,128)S(1)}, f32[4,512,128]{2,1,0:T(8,128)}, u32[]{:S(2)}) copy-start(f32[4,512,128]{2,1,0:T(8,128)} %get-tuple-element.30) | copy-start | bytes 3145732
  101.0 38.7 %copy-start.5 = (f32[4,512,128]{2,1,0:T(8,128)S(1)}, f32[4,512,128]{2,1,0:T(8,128)}, u32[]{:S(2)}) copy-start(f32[4,512,128]{2,1,0:T(8,128)} %get-tuple-element.24) | copy-start | bytes 3145732
  102.4 14.9 %collective-permute-start.7 = (f32[2,512,128]{2,1,0:T(8,128)S(1)}, f32[2,512,128]{2,1,0:T(8,128)S(1)}, u32[]{:S(2)}, u32[]{:S(2)}) collective-permute-start(f32[2,512,128]{2,1,0:T(8,128)S(1)} %slice_add_fusion.4), channel_id=1, source_target_pairs={{0,16},{8,24},{16,0},{24,8},{1,17},{9,25},{17,1},{25,9},{2,18},{10... | collective-permute-start | bytes 1572872 | tf_op jit(solution)/shard_map/ppermute | solution.py:25
  104.1 38.7 %collective-permute-start.19 = (f32[2,512,128]{2,1,0:T(8,128)S(1)}, f32[2,512,128]{2,1,0:T(8,128)S(1)}, u32[]{:S(2)}, u32[]{:S(2)}) collective-permute-start(f32[2,512,128]{2,1,0:T(8,128)S(1)} %slice_add_fusion), channel_id=1, source_target_pairs={{0,16},{8,24},{16,0},{24,8},{1,17},{9,25},{17,1},{25,9},{2,18},{10... | collective-permute-start | bytes 1572872 | tf_op jit(solution)/shard_map/ppermute | solution.py:25
  105.9 33.9 %collective-permute-start.3 = (f32[2,512,128]{2,1,0:T(8,128)S(1)}, f32[2,512,128]{2,1,0:T(8,128)S(1)}, u32[]{:S(2)}, u32[]{:S(2)}) collective-permute-start(f32[2,512,128]{2,1,0:T(8,128)S(1)} %slice_add_fusion.6), channel_id=1, source_target_pairs={{0,16},{8,24},{16,0},{24,8},{1,17},{9,25},{17,1},{25,9},{2,18},{10... | collective-permute-start | bytes 1572872 | tf_op jit(solution)/shard_map/ppermute | solution.py:25
  108.6 41.5 %collective-permute-start.17 = (f32[2,512,128]{2,1,0:T(8,128)S(1)}, f32[2,512,128]{2,1,0:T(8,128)S(1)}, u32[]{:S(2)}, u32[]{:S(2)}) collective-permute-start(f32[2,512,128]{2,1,0:T(8,128)S(1)} %slice_add_fusion.2), channel_id=1, source_target_pairs={{0,16},{8,24},{16,0},{24,8},{1,17},{9,25},{17,1},{25,9},{2,18},{10... | collective-permute-start | bytes 1572872 | tf_op jit(solution)/shard_map/ppermute | solution.py:25
  142.8 10.4 %collective-permute-start.8 = (f32[128,256]{1,0:T(8,128)S(1)}, f32[128,256]{1,0:T(8,128)S(1)}, u32[]{:S(2)}, u32[]{:S(2)}) collective-permute-start(f32[128,256]{1,0:T(8,128)S(1)} %slice_select_fusion.1), channel_id=1, source_target_pairs={{0,8},{8,0},{16,24},{24,16},{1,9},{9,1},{17,25},{25,17},{2,10},{10... | collective-permute-start | bytes 393224 | tf_op jit(solution)/shard_map/ppermute | solution.py:25
  153.1 12.0 %collective-permute-start.20 = (f32[128,256]{1,0:T(8,128)S(1)}, f32[128,256]{1,0:T(8,128)S(1)}, u32[]{:S(2)}, u32[]{:S(2)}) collective-permute-start(f32[128,256]{1,0:T(8,128)S(1)} %slice_select_fusion), channel_id=1, source_target_pairs={{0,8},{8,0},{16,24},{24,16},{1,9},{9,1},{17,25},{25,17},{2,10},{10... | collective-permute-start | bytes 393224 | tf_op jit(solution)/shard_map/ppermute | solution.py:25
  153.2 14.6 %collective-permute-start.9 = (f32[64,256]{1,0:T(8,128)S(1)}, f32[64,256]{1,0:T(8,128)S(1)}, u32[]{:S(2)}, u32[]{:S(2)}) collective-permute-start(f32[64,256]{1,0:T(8,128)S(1)} %slice_select_fusion.3), channel_id=1, source_target_pairs={{0,1},{1,0},{2,3},{3,2},{4,5},{5,4},{6,7},{7,6},{8,9},{9,8},{10,11... | collective-permute-start | bytes 196616 | tf_op jit(solution)/shard_map/ppermute | solution.py:25
  165.1 4.3 %collective-permute-start.21 = (f32[64,256]{1,0:T(8,128)S(1)}, f32[64,256]{1,0:T(8,128)S(1)}, u32[]{:S(2)}, u32[]{:S(2)}) collective-permute-start(f32[64,256]{1,0:T(8,128)S(1)} %slice_select_fusion.2), channel_id=1, source_target_pairs={{0,1},{1,0},{2,3},{3,2},{4,5},{5,4},{6,7},{7,6},{8,9},{9,8},{10,11... | collective-permute-start | bytes 196616 | tf_op jit(solution)/shard_map/ppermute | solution.py:25
  167.8 4.0 %collective-permute-start.10 = (f32[32,256]{1,0:T(8,128)S(1)}, f32[32,256]{1,0:T(8,128)S(1)}, u32[]{:S(2)}, u32[]{:S(2)}) collective-permute-start(f32[32,256]{1,0:T(8,128)S(1)} %slice_select_fusion.5), channel_id=1, source_target_pairs={{0,16},{8,24},{16,0},{24,8},{1,17},{9,25},{17,1},{25,9},{2,18},{10... | collective-permute-start | bytes 98312 | tf_op jit(solution)/shard_map/ppermute | solution.py:25
  169.5 4.0 %collective-permute-start.22 = (f32[32,256]{1,0:T(8,128)S(1)}, f32[32,256]{1,0:T(8,128)S(1)}, u32[]{:S(2)}, u32[]{:S(2)}) collective-permute-start(f32[32,256]{1,0:T(8,128)S(1)} %slice_select_fusion.4), channel_id=1, source_target_pairs={{0,16},{8,24},{16,0},{24,8},{1,17},{9,25},{17,1},{25,9},{2,18},{10... | collective-permute-start | bytes 98312 | tf_op jit(solution)/shard_map/ppermute | solution.py:25
  171.9 3.9 %collective-permute-start.11 = (f32[32,256]{1,0:T(8,128)S(1)}, f32[32,256]{1,0:T(8,128)S(1)}, u32[]{:S(2)}, u32[]{:S(2)}) collective-permute-start(f32[32,256]{1,0:T(8,128)S(1)} %select_add_fusion.5), channel_id=1, source_target_pairs={{0,2},{1,3},{2,0},{3,1},{4,6},{5,7},{6,4},{7,5},{8,10},{9,11},{10,... | collective-permute-start | bytes 98312 | tf_op jit(solution)/shard_map/ppermute | solution.py:25
  173.5 4.9 %collective-permute-start.23 = (f32[32,256]{1,0:T(8,128)S(1)}, f32[32,256]{1,0:T(8,128)S(1)}, u32[]{:S(2)}, u32[]{:S(2)}) collective-permute-start(f32[32,256]{1,0:T(8,128)S(1)} %select_add_fusion.4), channel_id=1, source_target_pairs={{0,2},{1,3},{2,0},{3,1},{4,6},{5,7},{6,4},{7,5},{8,10},{9,11},{10,... | collective-permute-start | bytes 98312 | tf_op jit(solution)/shard_map/ppermute | solution.py:25
  175.8 4.8 %collective-permute-start.12 = (f32[32,256]{1,0:T(8,128)S(1)}, f32[32,256]{1,0:T(8,128)S(1)}, u32[]{:S(2)}, u32[]{:S(2)}) collective-permute-start(f32[32,256]{1,0:T(8,128)S(1)} %add.75), channel_id=1, source_target_pairs={{0,4},{1,5},{2,6},{3,7},{4,0},{5,1},{6,2},{7,3},{8,12},{9,13},{10,... | collective-permute-start | bytes 98312 | tf_op jit(solution)/shard_map/ppermute | solution.py:25
  178.4 5.2 %collective-permute-start.24 = (f32[32,256]{1,0:T(8,128)S(1)}, f32[32,256]{1,0:T(8,128)S(1)}, u32[]{:S(2)}, u32[]{:S(2)}) collective-permute-start(f32[32,256]{1,0:T(8,128)S(1)} %add.86), channel_id=1, source_target_pairs={{0,4},{1,5},{2,6},{3,7},{4,0},{5,1},{6,2},{7,3},{8,12},{9,13},{10,... | collective-permute-start | bytes 98312 | tf_op jit(solution)/shard_map/ppermute | solution.py:25
  180.6 4.6 %collective-permute-start.13 = (f32[32,256]{1,0:T(8,128)S(1)}, f32[32,256]{1,0:T(8,128)S(1)}, u32[]{:S(2)}, u32[]{:S(2)}) collective-permute-start(f32[32,256]{1,0:T(8,128)S(1)} %add.76), channel_id=1, source_target_pairs={{0,16},{8,24},{16,0},{24,8},{1,17},{9,25},{17,1},{25,9},{2,18},{10... | collective-permute-start | bytes 98312 | tf_op jit(solution)/shard_map/ppermute | solution.py:25
  183.7 3.9 %collective-permute-start.25 = (f32[32,256]{1,0:T(8,128)S(1)}, f32[32,256]{1,0:T(8,128)S(1)}, u32[]{:S(2)}, u32[]{:S(2)}) collective-permute-start(f32[32,256]{1,0:T(8,128)S(1)} %add.87), channel_id=1, source_target_pairs={{0,16},{8,24},{16,0},{24,8},{1,17},{9,25},{17,1},{25,9},{2,18},{10... | collective-permute-start | bytes 98312 | tf_op jit(solution)/shard_map/ppermute | solution.py:25
  185.2 4.5 %collective-permute-start.14 = (f32[64,256]{1,0:T(8,128)S(1)}, f32[64,256]{1,0:T(8,128)S(1)}, u32[]{:S(2)}, u32[]{:S(2)}) collective-permute-start(f32[64,256]{1,0:T(8,128)S(1)} %maximum_select_fusion.4), channel_id=1, source_target_pairs={{0,1},{1,0},{2,3},{3,2},{4,5},{5,4},{6,7},{7,6},{8,9},{9,8},{10,11... | collective-permute-start | bytes 196616 | tf_op jit(solution)/shard_map/ppermute | solution.py:25
  187.6 4.4 %collective-permute-start.26 = (f32[64,256]{1,0:T(8,128)S(1)}, f32[64,256]{1,0:T(8,128)S(1)}, u32[]{:S(2)}, u32[]{:S(2)}) collective-permute-start(f32[64,256]{1,0:T(8,128)S(1)} %maximum_select_fusion.5), channel_id=1, source_target_pairs={{0,1},{1,0},{2,3},{3,2},{4,5},{5,4},{6,7},{7,6},{8,9},{9,8},{10,11... | collective-permute-start | bytes 196616 | tf_op jit(solution)/shard_map/ppermute | solution.py:25
  189.7 2.3 %collective-permute-start.15 = (f32[128,256]{1,0:T(8,128)S(1)}, f32[128,256]{1,0:T(8,128)S(1)}, u32[]{:S(2)}, u32[]{:S(2)}) collective-permute-start(f32[128,256]{1,0:T(8,128)S(1)} %maximum_select_fusion.2), channel_id=1, source_target_pairs={{0,8},{8,0},{16,24},{24,16},{1,9},{9,1},{17,25},{25,17},{2,10},{10... | collective-permute-start | bytes 393224 | tf_op jit(solution)/shard_map/ppermute | solution.py:25
  192.0 14.7 %collective-permute-start.27 = (f32[128,256]{1,0:T(8,128)S(1)}, f32[128,256]{1,0:T(8,128)S(1)}, u32[]{:S(2)}, u32[]{:S(2)}) collective-permute-start(f32[128,256]{1,0:T(8,128)S(1)} %maximum_select_fusion.3), channel_id=1, source_target_pairs={{0,8},{8,0},{16,24},{24,16},{1,9},{9,1},{17,25},{25,17},{2,10},{10... | collective-permute-start | bytes 393224 | tf_op jit(solution)/shard_map/ppermute | solution.py:25
  (4 other events, 3.2 us)

commit v4 on v3

--- a/solution.py
+++ b/solution.py
@@ -12,6 +12,7 @@
 LANES = 128
 AHEAD = 3
 STEP = 16
+PIECES = 2
 HIGHEST = lax.Precision.HIGHEST
 
 
@@ -350,37 +351,54 @@
     )(pole_values, source, inverse, coupled, arriving, added)
 
 
-def factor_kernel(total, gram_ref, y_ref, basis_ref, inverse_ref, acc):
-    n = gram_ref.shape[0]
-    rows = lax.broadcasted_iota(jnp.int32, (n, n), 0)
-    cols = lax.broadcasted_iota(jnp.int32, (n, n), 1)
-    acc[:, :n] = gram_ref[...] / total
-    acc[:, n:] = (rows == cols).astype(F32)
-    lane = 128
+def panel_kernel(total, start, stop, in_ref, acc):
+    n = acc.shape[0]
+    if start == 0:
+        rows = lax.broadcasted_iota(jnp.int32, (n, n), 0)
+        cols = lax.broadcasted_iota(jnp.int32, (n, n), 1)
+        acc[:, :n] = in_ref[...] / total
+        acc[:, n:] = (rows == cols).astype(F32)
+    else:
+        acc[...] = in_ref[...]
+    lane = min(LANES, n)
     row = lax.broadcasted_iota(jnp.int32, (STEP, lane), 0)
-    for r in range(0, n, STEP):
+
+    def spread(x):
+        return jnp.broadcast_to(x, (STEP, lane))
+
+    for r in range(start, stop, STEP):
         low = r // lane * lane
         high = (r + STEP + lane - 1) // lane * lane
         panel = acc[r : r + STEP, low : n + high]
-        tiles = [panel[:, i:i+lane] for i in range(0, panel.shape[1], lane)]
-        cols_ = [jnp.broadcast_to(panel[:, r-low+j:r-low+j+1], (STEP, lane)) for j in range(STEP)]
+        tiles = [panel[:, i : i + lane] for i in range(0, panel.shape[1], lane)]
+        columns = [spread(panel[:, r - low + j : r - low + j + 1]) for j in range(STEP)]
         scale = jnp.ones((STEP, lane), F32)
         for k in range(STEP):
-            inv = lax.rsqrt(jnp.broadcast_to(cols_[k][k:k+1], (STEP, lane)))
+            inv = lax.rsqrt(spread(columns[k][k : k + 1]))
             scale = jnp.where(row == k, inv, scale)
-            m = jnp.where(row > k, cols_[k], 0.0) * (inv * inv)
+            m = jnp.where(row > k, columns[k], 0.0) * (inv * inv)
             for j in range(k + 1, STEP):
-                cols_[j] = cols_[j] - m * jnp.broadcast_to(cols_[j][k:k+1], (STEP, lane))
-            tiles = [t - m * jnp.broadcast_to(t[k:k+1], (STEP, lane)) for t in tiles]
+                columns[j] = columns[j] - m * spread(columns[j][k : k + 1])
+            tiles = [t - m * spread(t[k : k + 1]) for t in tiles]
         done = jnp.concatenate([t * scale for t in tiles], axis=1)
         acc[r : r + STEP, low : n + high] = done
         if r + STEP < n:
-            left = done[:, :n-low].T[r+STEP-low:]
-            acc[r+STEP:, low : n + high] -= jnp.dot(left, done, precision=HIGHEST, preferred_element_type=F32)
-    inverse = jnp.where(cols <= rows, acc[:, n:], 0.0)
-    nt = (((1,), (1,)), ((), ()))
-    basis_ref[...] = lax.dot_general(y_ref[...], inverse, nt, precision=HIGHEST, preferred_element_type=F32)
+            left = done[:, : n - low].T[r + STEP - low :]
+            acc[r + STEP :, low : n + high] -= jnp.dot(
+                left, done, precision=HIGHEST, preferred_element_type=F32
+            )
+
+
+def basis_kernel(acc_ref, y_ref, basis_ref, inverse_ref):
+    n = acc_ref.shape[0]
+    rows = lax.broadcasted_iota(jnp.int32, (n, n), 0)
+    cols = lax.broadcasted_iota(jnp.int32, (n, n), 1)
+    inverse = jnp.where(cols <= rows, acc_ref[:, n:], 0.0)
     inverse_ref[...] = inverse
+    basis_ref[...] = lax.dot_general(
+        y_ref[...], inverse, (((1,), (1,)), ((), ())),
+        precision=HIGHEST, preferred_element_type=F32,
+    )
 
 
 def congruence_kernel(total, inverse_ref, proj_ref, ray_ref):
@@ -408,17 +426,29 @@
 def orthonormalized(total, gram, y):
     n = gram.shape[0]
     vmem = pl.BlockSpec(memory_space=pltpu.VMEM)
+    rows = n // PIECES
+    acc = gram
+    for p in range(PIECES):
+        acc = pl.pallas_call(
+            functools.partial(panel_kernel, float(total), p * rows, (p + 1) * rows),
+            out_shape=jax.ShapeDtypeStruct((n, 2 * n), F32),
+            in_specs=[vmem],
+            out_specs=vmem,
+            cost_estimate=pl.CostEstimate(
+                flops=2**31, transcendentals=0, bytes_accessed=2**20
+            ),
+            name="factor_panels",
+        )(acc)
     return pl.pallas_call(
-        functools.partial(factor_kernel, float(total)),
+        basis_kernel,
         out_shape=(jax.ShapeDtypeStruct(y.shape, F32), jax.ShapeDtypeStruct((n, n), F32)),
         in_specs=[vmem] * 2,
         out_specs=(vmem, vmem),
-        scratch_shapes=[pltpu.VMEM((n, 2 * n), F32)],
         cost_estimate=pl.CostEstimate(
-            flops=12 * 2**30, transcendentals=0, bytes_accessed=3 * 2**20
+            flops=2**31, transcendentals=0, bytes_accessed=3 * 2**20
         ),
-        name="orthonormalized",
-    )(gram, y)
+        name="basis",
+    )(acc, y)
 
 
 def inner_products(left, right_side):
@@ -440,8 +470,8 @@
         other = jnp.where(upper, x[:half], x[half:])
         x = mine + flipped(other, axis, 1 << i)
         kept.append(upper)
-    for axis, i in far:
-        x = x + flipped(x, axis, 1 << i)
+    axis, masks = far
+    x = x + sum(flipped(x, axis, mask) for mask in masks)
     for (axis, i), upper in zip(reversed(near), reversed(kept)):
         other = flipped(x, axis, 1 << i)
         x = jnp.where(upper, jnp.concatenate([other, x]), jnp.concatenate([x, other]))
@@ -491,7 +521,7 @@
     own_z = jnp.concatenate(own_z, axis=1)
     near = [("pole", i) for i in range(owners.bit_length() - 1)]
     near.insert(1, ("dom", 0))
-    far = [("dom", i) for i in range(1, parts.bit_length() - 1)]
+    far = ("dom", tuple(range(2, parts, 2)))
     gram = summed_everywhere(inner_products(own_y, own_y), near, far)
     projected = summed_everywhere(inner_products(own_y, own_z), near, far)
     row_total = blocks * order * parts

time: 211 us -> 215 us (1.019)
  Pallas kernels: 83.7 us -> 87.4 us
    pallas_call x1 -> x3, Pallas kernels: 13.9 us -> 17.6 us  [the longest x2 14.2 us: orthonormalized(): pl.pallas_call(functools.partial(panel_kernel, float(total), p * rows, (p...]
    ppermute x24 -> x26, waiting for transfers between devices: 43 us -> 43.6 us  [flipped(): lax.ppermute(x, axis, [(i, i ^ mask) for i in range(lax.axis_size(axis))])]
    ppermute x24 -> x26, starting transfers between devices: 36.9 us -> 36.6 us  [flipped(): lax.ppermute(x, axis, [(i, i ^ mask) for i in range(lax.axis_size(axis))])]
  transfers between devices with their start and end apart: 28 -> 30, of which waited for: 12 -> 11; matrix products, arithmetic and copies ran while one was open for 6% -> 6% of each run, Pallas kernels for 29% -> 31%
where the time goes in v4:
time: 215 us; the launch traced here: 214 us
  Pallas kernels  87.4 us (41%)
  waiting for transfers between devices  60.2 us (28%)
  starting transfers between devices  48.7 us (23%)
  other arithmetic  9.96 us (5%)
  matrix products  3.66 us (2%)
  local copies, waits for them, and re-layouts  3.25 us (2%)
    ppermute x26, waiting for transfers between devices, flipped(): lax.ppermute(x, axis, [(i, i ^ mask) for i in range(lax.axis_size(axis))])  43.6 us
    ppermute x26, starting transfers between devices, flipped(): lax.ppermute(x, axis, [(i, i ^ mask) for i in range(lax.axis_size(axis))])  36.6 us
    pallas_call x2, Pallas kernels, second_solve(): pl.pallas_call(functools.partial(second_kernel, chunk * width, owners), o...  34.8 us
    pallas_call x1, Pallas kernels, first_solve(): pl.pallas_call(functools.partial(first_kernel, groups), out_shape=(tip,)...  19.1 us
    ppermute x4, waiting for transfers between devices, shifted(): return lax.ppermute(x, axis, pairs)  16.7 us
    pallas_call x2, Pallas kernels, orthonormalized(): pl.pallas_call(functools.partial(panel_kernel, float(total), p * rows, (p...  14.2 us
    ppermute x4, starting transfers between devices, shifted(): return lax.ppermute(x, axis, pairs)  12.1 us
    pallas_call x2, Pallas kernels, interface_above(): pl.pallas_call(functools.partial(above_kernel, parts), out_shape=jax.Shap...  6.68 us
  transfers between devices with their start and end apart: 30, of which 11 were waited for; matrix products, arithmetic and copies ran while one was open for 6% of the time, Pallas kernels for 31%

profile of v4, /device:TPU:0, one launch (start us, length us, event | category | flops | bytes accessed | tf_op | source)
XLA Modules:
  0.0 214.2 jit_solution(6018125294924885689)
XLA Ops:
  0.6 19.1 %first_solve.1 = (f32[512,256]{1,0:T(8,128)}, f32[512,256]{1,0:T(8,128)}, f32[512,256]{1,0:T(8,128)}, f32[512,256]{1,0:T(8,128)}) custom-call(bf16[8,512,256]{2,1,0:T(8,128)(2,1)} %bitcast.32, bf16[8,1024,512]{2,1,0:T(8,128)(2,1)} %bitcast.29, bf16[8,512,512]{2,1,0:T(8,128)(2,1)} %bitcast.9, bf16[3,1024,512]{2,1,0:T(8,128)(2,1)} %bitcast.16), custom_call_target="tpu_custom_call" | custom-call | flops 9932111872 | bytes 14680064 | tf_op jit(solution)/shard_map/first_solve/pallas_call | solution.py:126
  22.3 15.3 %collective-permute-done.4.next_hbm = f32[512,256]{1,0:T(8,128)S(1)} collective-permute-done((f32[512,256]{1,0:T(8,128)}, f32[512,256]{1,0:T(8,128)S(1)}, u32[]{:S(2)}, u32[]{:S(2)}) %collective-permute-start.4) | collective-permute-done | bytes 524320 | tf_op jit(solution)/shard_map/ppermute | solution.py:22
  38.4 3.3 %interface_below.3 = (f32[512,256]{1,0:T(8,128)}, f32[512,256]{1,0:T(8,128)}) custom-call(f32[512,256]{1,0:T(8,128)} %get-tuple-element.26.sb_hbm, f32[512,256]{1,0:T(8,128)} %copy-done.1, bf16[3,1024,512]{2,1,0:T(8,128)(2,1)} %bitcast.17, bf16[8,512,512]{2,1,0:T(8,128)(2,1)} %bitcast.10), custom_call_target="tpu_custom_call" | custom-call | flops 402653184 | bytes 4194304 | tf_op jit(solution)/shard_map/interface_below/pallas_call | solution.py:171
  41.7 4.8 %collective-permute-start.5 = (f32[512,256]{1,0:T(8,128)}, f32[512,256]{1,0:T(8,128)S(1)}, u32[]{:S(2)}, u32[]{:S(2)}) collective-permute-start(f32[512,256]{1,0:T(8,128)} %get-tuple-element.28), channel_id=1, source_target_pairs={{0,1},{1,2},{2,3},{3,4},{4,5},{5,6},{6,7},{8,9},{9,10},{10,11},{11... | collective-permute-start | bytes 1572872 | tf_op jit(solution)/shard_map/ppermute | solution.py:22
  48.7 3.3 %interface_below.2 = (f32[512,256]{1,0:T(8,128)}, f32[512,256]{1,0:T(8,128)}) custom-call(f32[512,256]{1,0:T(8,128)} %get-tuple-element.20.sb_hbm, f32[512,256]{1,0:T(8,128)} %copy-done, bf16[3,1024,512]{2,1,0:T(8,128)(2,1)} %bitcast.18, bf16[8,512,512]{2,1,0:T(8,128)(2,1)} %bitcast.11), custom_call_target="tpu_custom_call" | custom-call | flops 402653184 | bytes 4194304 | tf_op jit(solution)/shard_map/interface_below/pallas_call | solution.py:171
  52.0 4.7 %collective-permute-start.1 = (f32[512,256]{1,0:T(8,128)}, f32[512,256]{1,0:T(8,128)S(1)}, u32[]{:S(2)}, u32[]{:S(2)}) collective-permute-start(f32[512,256]{1,0:T(8,128)} %get-tuple-element.22), channel_id=1, source_target_pairs={{0,1},{1,2},{2,3},{3,4},{4,5},{5,6},{6,7},{8,9},{9,10},{10,11},{11... | collective-permute-start | bytes 1572872 | tf_op jit(solution)/shard_map/ppermute | solution.py:22
  56.7 3.3 %interface_above.3.added_hbm = f32[512,256]{1,0:T(8,128)} custom-call(f32[512,256]{1,0:T(8,128)} %get-tuple-element.29.below_hbm, f32[512,256]{1,0:T(8,128)} %copy-done.1, bf16[3,1024,512]{2,1,0:T(8,128)(2,1)} %bitcast.19, bf16[8,512,512]{2,1,0:T(8,128)(2,1)} %bitcast.12), custom_call_target="tpu_custom_call" | custom-call | flops 402653184 | bytes 4194304 | tf_op jit(solution)/shard_map/interface_above/pallas_call | solution.py:212
  60.8 17.4 %second_solve.3 = (f32[4,512,128]{2,1,0:T(8,128)}, f32[4,512,128]{2,1,0:T(8,128)}, f32[4,512,128]{2,1,0:T(8,128)}, f32[4,512,128]{2,1,0:T(8,128)}) custom-call(f32[1,4]{1,0:T(1,128)} %pole_ref.3, bf16[8,512,256]{2,1,0:T(8,128)(2,1)} %bitcast.33, bf16[8,1024,512]{2,1,0:T(8,128)(2,1)} %bitcast.30, bf16[8,512,512]{2,1,0:T(8,128)(2,1)} %bitcast.13, ...), custom_call_target="tpu_custom_call" | custom-call | flops 4966055936 | bytes 16777216 | tf_op jit(solution)/shard_map/second_solve/pallas_call | solution.py:330
  78.3 3.4 %interface_above.2.added_hbm = f32[512,256]{1,0:T(8,128)} custom-call(f32[512,256]{1,0:T(8,128)} %get-tuple-element.23.below_hbm, f32[512,256]{1,0:T(8,128)} %copy-done, bf16[3,1024,512]{2,1,0:T(8,128)(2,1)} %bitcast.20, bf16[8,512,512]{2,1,0:T(8,128)(2,1)} %bitcast.14), custom_call_target="tpu_custom_call" | custom-call | flops 402653184 | bytes 4194304 | tf_op jit(solution)/shard_map/interface_above/pallas_call | solution.py:212
  83.1 17.4 %second_solve.2 = (f32[4,512,128]{2,1,0:T(8,128)}, f32[4,512,128]{2,1,0:T(8,128)}, f32[4,512,128]{2,1,0:T(8,128)}, f32[4,512,128]{2,1,0:T(8,128)}) custom-call(f32[1,4]{1,0:T(1,128)} %pole_ref.3, bf16[8,512,256]{2,1,0:T(8,128)(2,1)} %bitcast.34, bf16[8,1024,512]{2,1,0:T(8,128)(2,1)} %bitcast.31, bf16[8,512,512]{2,1,0:T(8,128)(2,1)} %bitcast.15, ...), custom_call_target="tpu_custom_call" | custom-call | flops 4966055936 | bytes 16777216 | tf_op jit(solution)/shard_map/second_solve/pallas_call | solution.py:330
  102.5 1.6 collective-permute-start.7
  105.9 1.6 collective-permute-start.3
  109.2 8.1 %collective-permute-done.7 = f32[2,512,128]{2,1,0:T(8,128)S(1)} collective-permute-done((f32[2,512,128]{2,1,0:T(8,128)S(1)}, f32[2,512,128]{2,1,0:T(8,128)S(1)}, u32[]{:S(2)}, u32[]{:S(2)}) %collective-permute-start.7) | collective-permute-done | bytes 524320 | tf_op jit(solution)/shard_map/ppermute | solution.py:26
  118.4 21.4 %collective-permute-done.3 = f32[2,512,128]{2,1,0:T(8,128)S(1)} collective-permute-done((f32[2,512,128]{2,1,0:T(8,128)S(1)}, f32[2,512,128]{2,1,0:T(8,128)S(1)}, u32[]{:S(2)}, u32[]{:S(2)}) %collective-permute-start.3) | collective-permute-done | bytes 524320 | tf_op jit(solution)/shard_map/ppermute | solution.py:26
  140.9 1.8 fusion.9
  143.0 7.2 %collective-permute-done.18 = f32[2,512,128]{2,1,0:T(8,128)S(1)} collective-permute-done((f32[2,512,128]{2,1,0:T(8,128)S(1)}, f32[2,512,128]{2,1,0:T(8,128)S(1)}, u32[]{:S(2)}, u32[]{:S(2)}) %collective-permute-start.18) | collective-permute-done | bytes 524320 | tf_op jit(solution)/shard_map/ppermute | solution.py:26
  151.3 1.8 fusion
  153.3 11.8 %collective-permute-start.9 = (f32[64,256]{1,0:T(8,128)S(1)}, f32[64,256]{1,0:T(8,128)S(1)}, u32[]{:S(2)}, u32[]{:S(2)}) collective-permute-start(f32[64,256]{1,0:T(8,128)S(1)} %slice_select_fusion.3), channel_id=1, source_target_pairs={{0,1},{1,0},{2,3},{3,2},{4,5},{5,4},{6,7},{7,6},{8,9},{9,8},{10,11... | collective-permute-start | bytes 196616 | tf_op jit(solution)/shard_map/ppermute | solution.py:26
  166.4 1.4 collective-permute-done.9
  167.8 1.6 collective-permute-start.10
  169.5 1.6 collective-permute-start.23
  171.9 2.7 %collective-permute-start.13 = (f32[32,256]{1,0:T(8,128)S(1)}, f32[32,256]{1,0:T(8,128)S(1)}, u32[]{:S(2)}, u32[]{:S(2)}) collective-permute-start(f32[32,256]{1,0:T(8,128)S(1)} %select_add_fusion.5), channel_id=1, source_target_pairs={{0,6},{1,7},{2,4},{3,5},{4,2},{5,3},{6,0},{7,1},{8,14},{9,15},{10,... | collective-permute-start | bytes 98312 | tf_op jit(solution)/shard_map/ppermute | solution.py:26
  176.3 2.8 %collective-permute-start.26 = (f32[32,256]{1,0:T(8,128)S(1)}, f32[32,256]{1,0:T(8,128)S(1)}, u32[]{:S(2)}, u32[]{:S(2)}) collective-permute-start(f32[32,256]{1,0:T(8,128)S(1)} %select_add_fusion.4), channel_id=1, source_target_pairs={{0,6},{1,7},{2,4},{3,5},{4,2},{5,3},{6,0},{7,1},{8,14},{9,15},{10,... | collective-permute-start | bytes 98312 | tf_op jit(solution)/shard_map/ppermute | solution.py:26
  179.1 1.7 collective-permute-start.24
  180.8 1.6 collective-permute-start.14
  182.4 1.5 collective-permute-done.25
  183.9 1.6 collective-permute-start.27
  185.5 1.5 collective-permute-start.15
  193.1 7.8 %factor_panels.2.in_ref = f32[256,512]{1,0:T(8,128)} custom-call(f32[256,256]{1,0:T(8,128)} %maximum_select_fusion.in_ref), custom_call_target="tpu_custom_call" | custom-call | flops 2147483648 | bytes 1048576 | tf_op jit(solution)/shard_map/factor_panels/pallas_call | solution.py:432
  200.9 6.4 %factor_panels.3.acc_ref = f32[256,512]{1,0:T(8,128)} custom-call(f32[256,512]{1,0:T(8,128)} %factor_panels.2.in_ref), custom_call_target="tpu_custom_call" | custom-call | flops 2147483648 | bytes 1048576 | tf_op jit(solution)/shard_map/factor_panels/pallas_call | solution.py:432
  207.3 3.4 %basis.1 = (f32[1024,256]{1,0:T(8,128)}, f32[256,256]{1,0:T(8,128)}) custom-call(f32[256,512]{1,0:T(8,128)} %factor_panels.3.acc_ref, f32[1024,256]{1,0:T(8,128)} %pad_maximum_fusion.y_ref), custom_call_target="tpu_custom_call" | custom-call | flops 2147483648 | bytes 3145728 | tf_op jit(solution)/shard_map/basis/pallas_call | solution.py:442
  211.4 2.7 %congruence.1 = f32[256,256]{1,0:T(8,128)} custom-call(f32[256,256]{1,0:T(8,128)} %get-tuple-element.33.inverse_ref, f32[256,256]{1,0:T(8,128)} %maximum_select_fusion.1.proj_ref), custom_call_target="tpu_custom_call" | custom-call | flops 1073741824 | bytes 1048576 | tf_op jit(solution)/shard_map/congruence/pallas_call | solution.py:416
  (86 shorter events, 27.7 us)
Async XLA Ops:
  19.7 17.9 %collective-permute-start.4 = (f32[512,256]{1,0:T(8,128)}, f32[512,256]{1,0:T(8,128)S(1)}, u32[]{:S(2)}, u32[]{:S(2)}) collective-permute-start(f32[512,256]{1,0:T(8,128)} %get-tuple-element.27), channel_id=1, source_target_pairs={{1,0},{2,1},{3,2},{4,3},{5,4},{6,5},{7,6},{9,8},{10,9},{11,10},{12... | collective-permute-start | bytes 1572872 | tf_op jit(solution)/shard_map/ppermute | solution.py:22
  21.0 26.9 %collective-permute-start = (f32[512,256]{1,0:T(8,128)}, f32[512,256]{1,0:T(8,128)S(1)}, u32[]{:S(2)}, u32[]{:S(2)}) collective-permute-start(f32[512,256]{1,0:T(8,128)} %get-tuple-element.21), channel_id=1, source_target_pairs={{1,0},{2,1},{3,2},{4,3},{5,4},{6,5},{7,6},{9,8},{10,9},{11,10},{12... | collective-permute-start | bytes 1572872 | tf_op jit(solution)/shard_map/ppermute | solution.py:22
  41.7 18.3 %collective-permute-start.5 = (f32[512,256]{1,0:T(8,128)}, f32[512,256]{1,0:T(8,128)S(1)}, u32[]{:S(2)}, u32[]{:S(2)}) collective-permute-start(f32[512,256]{1,0:T(8,128)} %get-tuple-element.28), channel_id=1, source_target_pairs={{0,1},{1,2},{2,3},{3,4},{4,5},{5,6},{6,7},{8,9},{9,10},{10,11},{11... | collective-permute-start | bytes 1572872 | tf_op jit(solution)/shard_map/ppermute | solution.py:22
  52.0 30.2 %collective-permute-start.1 = (f32[512,256]{1,0:T(8,128)}, f32[512,256]{1,0:T(8,128)S(1)}, u32[]{:S(2)}, u32[]{:S(2)}) collective-permute-start(f32[512,256]{1,0:T(8,128)} %get-tuple-element.22), channel_id=1, source_target_pairs={{0,1},{1,2},{2,3},{3,4},{4,5},{5,6},{6,7},{8,9},{9,10},{10,11},{11... | collective-permute-start | bytes 1572872 | tf_op jit(solution)/shard_map/ppermute | solution.py:22
  78.2 22.8 %collective-permute-start.6 = (f32[4,512,128]{2,1,0:T(8,128)}, f32[4,512,128]{2,1,0:T(8,128)}, u32[]{:S(2)}, u32[]{:S(2)}) collective-permute-start(f32[4,512,128]{2,1,0:T(8,128)} %get-tuple-element.31), channel_id=1, source_target_pairs={{0,8},{8,0},{16,24},{24,16},{1,9},{9,1},{17,25},{25,17},{2,10},{10... | collective-permute-start | bytes 3145736 | tf_op jit(solution)/shard_map/ppermute | solution.py:26
  81.7 22.4 %copy-start.2 = (f32[4,512,128]{2,1,0:T(8,128)S(1)}, f32[4,512,128]{2,1,0:T(8,128)}, u32[]{:S(2)}) copy-start(f32[4,512,128]{2,1,0:T(8,128)} %get-tuple-element.36) | copy-start | bytes 3145732
  81.7 22.4 %collective-permute-start.19 = (f32[4,512,128]{2,1,0:T(8,128)}, f32[4,512,128]{2,1,0:T(8,128)S(1)}, u32[]{:S(2)}, u32[]{:S(2)}) collective-permute-start(f32[4,512,128]{2,1,0:T(8,128)} %get-tuple-element.37), channel_id=1, source_target_pairs={{0,8},{8,0},{16,24},{24,16},{1,9},{9,1},{17,25},{25,17},{2,10},{10... | collective-permute-start | bytes 3145736 | tf_op jit(solution)/shard_map/ppermute | solution.py:26
  100.5 4.2 %collective-permute-start.2 = (f32[4,512,128]{2,1,0:T(8,128)}, f32[4,512,128]{2,1,0:T(8,128)}, u32[]{:S(2)}, u32[]{:S(2)}) collective-permute-start(f32[4,512,128]{2,1,0:T(8,128)} %get-tuple-element.25), channel_id=1, source_target_pairs={{0,8},{8,0},{16,24},{24,16},{1,9},{9,1},{17,25},{25,17},{2,10},{10... | collective-permute-start | bytes 3145736 | tf_op jit(solution)/shard_map/ppermute | solution.py:26
  100.5 7.0 %collective-permute-start.17 = (f32[4,512,128]{2,1,0:T(8,128)}, f32[4,512,128]{2,1,0:T(8,128)}, u32[]{:S(2)}, u32[]{:S(2)}) collective-permute-start(f32[4,512,128]{2,1,0:T(8,128)} %get-tuple-element.35), channel_id=1, source_target_pairs={{0,8},{8,0},{16,24},{24,16},{1,9},{9,1},{17,25},{25,17},{2,10},{10... | collective-permute-start | bytes 3145736 | tf_op jit(solution)/shard_map/ppermute | solution.py:26
  101.0 38.7 %copy-start.5 = (f32[4,512,128]{2,1,0:T(8,128)S(1)}, f32[4,512,128]{2,1,0:T(8,128)}, u32[]{:S(2)}) copy-start(f32[4,512,128]{2,1,0:T(8,128)} %get-tuple-element.24) | copy-start | bytes 3145732
  102.5 14.9 %collective-permute-start.7 = (f32[2,512,128]{2,1,0:T(8,128)S(1)}, f32[2,512,128]{2,1,0:T(8,128)S(1)}, u32[]{:S(2)}, u32[]{:S(2)}) collective-permute-start(f32[2,512,128]{2,1,0:T(8,128)S(1)} %slice_add_fusion.4), channel_id=1, source_target_pairs={{0,16},{8,24},{16,0},{24,8},{1,17},{9,25},{17,1},{25,9},{2,18},{10... | collective-permute-start | bytes 1572872 | tf_op jit(solution)/shard_map/ppermute | solution.py:26
  104.1 38.8 %collective-permute-start.20 = (f32[2,512,128]{2,1,0:T(8,128)S(1)}, f32[2,512,128]{2,1,0:T(8,128)S(1)}, u32[]{:S(2)}, u32[]{:S(2)}) collective-permute-start(f32[2,512,128]{2,1,0:T(8,128)S(1)} %slice_add_fusion), channel_id=1, source_target_pairs={{0,16},{8,24},{16,0},{24,8},{1,17},{9,25},{17,1},{25,9},{2,18},{10... | collective-permute-start | bytes 1572872 | tf_op jit(solution)/shard_map/ppermute | solution.py:26
  105.9 33.9 %collective-permute-start.3 = (f32[2,512,128]{2,1,0:T(8,128)S(1)}, f32[2,512,128]{2,1,0:T(8,128)S(1)}, u32[]{:S(2)}, u32[]{:S(2)}) collective-permute-start(f32[2,512,128]{2,1,0:T(8,128)S(1)} %slice_add_fusion.6), channel_id=1, source_target_pairs={{0,16},{8,24},{16,0},{24,8},{1,17},{9,25},{17,1},{25,9},{2,18},{10... | collective-permute-start | bytes 1572872 | tf_op jit(solution)/shard_map/ppermute | solution.py:26
  108.6 41.5 %collective-permute-start.18 = (f32[2,512,128]{2,1,0:T(8,128)S(1)}, f32[2,512,128]{2,1,0:T(8,128)S(1)}, u32[]{:S(2)}, u32[]{:S(2)}) collective-permute-start(f32[2,512,128]{2,1,0:T(8,128)S(1)} %slice_add_fusion.2), channel_id=1, source_target_pairs={{0,16},{8,24},{16,0},{24,8},{1,17},{9,25},{17,1},{25,9},{2,18},{10... | collective-permute-start | bytes 1572872 | tf_op jit(solution)/shard_map/ppermute | solution.py:26
  142.8 10.4 %collective-permute-start.8 = (f32[128,256]{1,0:T(8,128)S(1)}, f32[128,256]{1,0:T(8,128)S(1)}, u32[]{:S(2)}, u32[]{:S(2)}) collective-permute-start(f32[128,256]{1,0:T(8,128)S(1)} %slice_select_fusion.1), channel_id=1, source_target_pairs={{0,8},{8,0},{16,24},{24,16},{1,9},{9,1},{17,25},{25,17},{2,10},{10... | collective-permute-start | bytes 393224 | tf_op jit(solution)/shard_map/ppermute | solution.py:26
  153.1 12.0 %collective-permute-start.21 = (f32[128,256]{1,0:T(8,128)S(1)}, f32[128,256]{1,0:T(8,128)S(1)}, u32[]{:S(2)}, u32[]{:S(2)}) collective-permute-start(f32[128,256]{1,0:T(8,128)S(1)} %slice_select_fusion), channel_id=1, source_target_pairs={{0,8},{8,0},{16,24},{24,16},{1,9},{9,1},{17,25},{25,17},{2,10},{10... | collective-permute-start | bytes 393224 | tf_op jit(solution)/shard_map/ppermute | solution.py:26
  153.3 14.6 %collective-permute-start.9 = (f32[64,256]{1,0:T(8,128)S(1)}, f32[64,256]{1,0:T(8,128)S(1)}, u32[]{:S(2)}, u32[]{:S(2)}) collective-permute-start(f32[64,256]{1,0:T(8,128)S(1)} %slice_select_fusion.3), channel_id=1, source_target_pairs={{0,1},{1,0},{2,3},{3,2},{4,5},{5,4},{6,7},{7,6},{8,9},{9,8},{10,11... | collective-permute-start | bytes 196616 | tf_op jit(solution)/shard_map/ppermute | solution.py:26
  165.1 4.3 %collective-permute-start.22 = (f32[64,256]{1,0:T(8,128)S(1)}, f32[64,256]{1,0:T(8,128)S(1)}, u32[]{:S(2)}, u32[]{:S(2)}) collective-permute-start(f32[64,256]{1,0:T(8,128)S(1)} %slice_select_fusion.2), channel_id=1, source_target_pairs={{0,1},{1,0},{2,3},{3,2},{4,5},{5,4},{6,7},{7,6},{8,9},{9,8},{10,11... | collective-permute-start | bytes 196616 | tf_op jit(solution)/shard_map/ppermute | solution.py:26
  167.8 4.1 %collective-permute-start.10 = (f32[32,256]{1,0:T(8,128)S(1)}, f32[32,256]{1,0:T(8,128)S(1)}, u32[]{:S(2)}, u32[]{:S(2)}) collective-permute-start(f32[32,256]{1,0:T(8,128)S(1)} %slice_select_fusion.5), channel_id=1, source_target_pairs={{0,16},{8,24},{16,0},{24,8},{1,17},{9,25},{17,1},{25,9},{2,18},{10... | collective-permute-start | bytes 98312 | tf_op jit(solution)/shard_map/ppermute | solution.py:26
  169.5 6.8 %collective-permute-start.23 = (f32[32,256]{1,0:T(8,128)S(1)}, f32[32,256]{1,0:T(8,128)S(1)}, u32[]{:S(2)}, u32[]{:S(2)}) collective-permute-start(f32[32,256]{1,0:T(8,128)S(1)} %slice_select_fusion.4), channel_id=1, source_target_pairs={{0,16},{8,24},{16,0},{24,8},{1,17},{9,25},{17,1},{25,9},{2,18},{10... | collective-permute-start | bytes 98312 | tf_op jit(solution)/shard_map/ppermute | solution.py:26
  171.9 7.2 %collective-permute-start.13 = (f32[32,256]{1,0:T(8,128)S(1)}, f32[32,256]{1,0:T(8,128)S(1)}, u32[]{:S(2)}, u32[]{:S(2)}) collective-permute-start(f32[32,256]{1,0:T(8,128)S(1)} %select_add_fusion.5), channel_id=1, source_target_pairs={{0,6},{1,7},{2,4},{3,5},{4,2},{5,3},{6,0},{7,1},{8,14},{9,15},{10,... | collective-permute-start | bytes 98312 | tf_op jit(solution)/shard_map/ppermute | solution.py:26
  174.6 6.1 %collective-permute-start.12 = (f32[32,256]{1,0:T(8,128)S(1)}, f32[32,256]{1,0:T(8,128)S(1)}, u32[]{:S(2)}, u32[]{:S(2)}) collective-permute-start(f32[32,256]{1,0:T(8,128)S(1)} %select_add_fusion.5), channel_id=1, source_target_pairs={{0,4},{1,5},{2,6},{3,7},{4,0},{5,1},{6,2},{7,3},{8,12},{9,13},{10,... | collective-permute-start | bytes 98312 | tf_op jit(solution)/shard_map/ppermute | solution.py:26
  174.9 5.8 %collective-permute-start.11 = (f32[32,256]{1,0:T(8,128)S(1)}, f32[32,256]{1,0:T(8,128)S(1)}, u32[]{:S(2)}, u32[]{:S(2)}) collective-permute-start(f32[32,256]{1,0:T(8,128)S(1)} %select_add_fusion.5), channel_id=1, source_target_pairs={{0,2},{1,3},{2,0},{3,1},{4,6},{5,7},{6,4},{7,5},{8,10},{9,11},{10,... | collective-permute-start | bytes 98312 | tf_op jit(solution)/shard_map/ppermute | solution.py:26
  176.3 6.1 %collective-permute-start.26 = (f32[32,256]{1,0:T(8,128)S(1)}, f32[32,256]{1,0:T(8,128)S(1)}, u32[]{:S(2)}, u32[]{:S(2)}) collective-permute-start(f32[32,256]{1,0:T(8,128)S(1)} %select_add_fusion.4), channel_id=1, source_target_pairs={{0,6},{1,7},{2,4},{3,5},{4,2},{5,3},{6,0},{7,1},{8,14},{9,15},{10,... | collective-permute-start | bytes 98312 | tf_op jit(solution)/shard_map/ppermute | solution.py:26
  179.1 4.8 %collective-permute-start.25 = (f32[32,256]{1,0:T(8,128)S(1)}, f32[32,256]{1,0:T(8,128)S(1)}, u32[]{:S(2)}, u32[]{:S(2)}) collective-permute-start(f32[32,256]{1,0:T(8,128)S(1)} %select_add_fusion.4), channel_id=1, source_target_pairs={{0,4},{1,5},{2,6},{3,7},{4,0},{5,1},{6,2},{7,3},{8,12},{9,13},{10,... | collective-permute-start | bytes 98312 | tf_op jit(solution)/shard_map/ppermute | solution.py:26
  179.1 4.8 %collective-permute-start.24 = (f32[32,256]{1,0:T(8,128)S(1)}, f32[32,256]{1,0:T(8,128)S(1)}, u32[]{:S(2)}, u32[]{:S(2)}) collective-permute-start(f32[32,256]{1,0:T(8,128)S(1)} %select_add_fusion.4), channel_id=1, source_target_pairs={{0,2},{1,3},{2,0},{3,1},{4,6},{5,7},{6,4},{7,5},{8,10},{9,11},{10,... | collective-permute-start | bytes 98312 | tf_op jit(solution)/shard_map/ppermute | solution.py:26
  180.8 4.7 %collective-permute-start.14 = (f32[32,256]{1,0:T(8,128)S(1)}, f32[32,256]{1,0:T(8,128)S(1)}, u32[]{:S(2)}, u32[]{:S(2)}) collective-permute-start(f32[32,256]{1,0:T(8,128)S(1)} %add_add_fusion.1), channel_id=1, source_target_pairs={{0,16},{8,24},{16,0},{24,8},{1,17},{9,25},{17,1},{25,9},{2,18},{10... | collective-permute-start | bytes 98312 | tf_op jit(solution)/shard_map/ppermute | solution.py:26
  183.9 4.0 %collective-permute-start.27 = (f32[32,256]{1,0:T(8,128)S(1)}, f32[32,256]{1,0:T(8,128)S(1)}, u32[]{:S(2)}, u32[]{:S(2)}) collective-permute-start(f32[32,256]{1,0:T(8,128)S(1)} %add_add_fusion), channel_id=1, source_target_pairs={{0,16},{8,24},{16,0},{24,8},{1,17},{9,25},{17,1},{25,9},{2,18},{10... | collective-permute-start | bytes 98312 | tf_op jit(solution)/shard_map/ppermute | solution.py:26
  185.5 4.3 %collective-permute-start.15 = (f32[64,256]{1,0:T(8,128)S(1)}, f32[64,256]{1,0:T(8,128)S(1)}, u32[]{:S(2)}, u32[]{:S(2)}) collective-permute-start(f32[64,256]{1,0:T(8,128)S(1)} %maximum_select_fusion.4), channel_id=1, source_target_pairs={{0,1},{1,0},{2,3},{3,2},{4,5},{5,4},{6,7},{7,6},{8,9},{9,8},{10,11... | collective-permute-start | bytes 196616 | tf_op jit(solution)/shard_map/ppermute | solution.py:26
  187.9 4.3 %collective-permute-start.28 = (f32[64,256]{1,0:T(8,128)S(1)}, f32[64,256]{1,0:T(8,128)S(1)}, u32[]{:S(2)}, u32[]{:S(2)}) collective-permute-start(f32[64,256]{1,0:T(8,128)S(1)} %maximum_select_fusion.5), channel_id=1, source_target_pairs={{0,1},{1,0},{2,3},{3,2},{4,5},{5,4},{6,7},{7,6},{8,9},{9,8},{10,11... | collective-permute-start | bytes 196616 | tf_op jit(solution)/shard_map/ppermute | solution.py:26
  189.9 2.5 %collective-permute-start.16 = (f32[128,256]{1,0:T(8,128)S(1)}, f32[128,256]{1,0:T(8,128)S(1)}, u32[]{:S(2)}, u32[]{:S(2)}) collective-permute-start(f32[128,256]{1,0:T(8,128)S(1)} %maximum_select_fusion.2), channel_id=1, source_target_pairs={{0,8},{8,0},{16,24},{24,16},{1,9},{9,1},{17,25},{25,17},{2,10},{10... | collective-permute-start | bytes 393224 | tf_op jit(solution)/shard_map/ppermute | solution.py:26
  192.3 18.4 %collective-permute-start.29 = (f32[128,256]{1,0:T(8,128)S(1)}, f32[128,256]{1,0:T(8,128)S(1)}, u32[]{:S(2)}, u32[]{:S(2)}) collective-permute-start(f32[128,256]{1,0:T(8,128)S(1)} %maximum_select_fusion.3), channel_id=1, source_target_pairs={{0,8},{8,0},{16,24},{24,16},{1,9},{9,1},{17,25},{25,17},{2,10},{10... | collective-permute-start | bytes 393224 | tf_op jit(solution)/shard_map/ppermute | solution.py:26
  (6 other events, 26.6 us)
